TPU v7x, 128 devices: a whole 4x4x4 slice. The times are simulated.
128 devices in a mesh: area: 16 (over z_lo, y, core), layer: 8 (over z_hi, x).
Axes of the slice: x: 4, y: 4, z: 4 (z_hi: 2, z_lo: 2; z = z_hi * 2 + z_lo), core: 2. Of those that a mesh axis runs over, the one named last changes fastest.
Arguments:
- permeability: float32 [32, 8192, 512], P('layer', 'area'), may hold values from 0.1 to 10
- mobility: float32 [32, 8192, 512], P('layer', 'area'), may hold values from 0.3 to 3
- thickness: float32 [32], P('layer'), may hold values from 0.5 to 2
- caprock: int32 [8192, 512], P('area'), may hold values from 0 to 15
- plume: int32 [8192, 512], P('area'), may hold values from 0 to 31
- storage: float32 [8192, 512], P('area'), may hold values from 3.2 to 32
- source: float32 [8192, 512], P('area'), may hold values from -384 to 384
- pressure_old: float32 [8192, 512], P('area'), may hold values from -6 to 6
Outputs:
- cell_pressure: float32 [32, 8192, 512], P('layer', 'area')
- flux_rows: float32 [32, 8192, 512], P('layer', 'area')
- flux_cols: float32 [32, 8192, 512], P('layer', 'area')
Inputs may be any that keep to these rules, and one draw needn't show every extreme that they name: Layers above layer caprock of a column are sealed rock. CO2 fills the open layers above layer plume of a column; where plume <= caprock a column holds no CO2.
All inputs are finite; a program needn't handle non-finite values.
Results may differ from a plain program's by a relative error of at most 0.0003.
Values sent between devices are 32-bit elements; how exact they have to be, the bound alone decides.
A program may use at most 128 MiB of HBM per device.

v0:
```python
import jax
import jax.numpy as jnp
from jax import lax
from jax.sharding import PartitionSpec as P

SWEEPS = 3


buoyancy_scale = 0.3
gravity_scale = 0.05
gas_density = 0.7
brine_density = 1.0


def from_everyone(array, axis):
    copies = jnp.broadcast_to(array, (lax.axis_size(axis), *array.shape))
    return lax.all_to_all(copies, axis, split_axis=0, concat_axis=0, tiled=True)


def laid_out(blocks, dim):
    blocks = jnp.moveaxis(blocks, 0, dim)
    shape = blocks.shape
    return blocks.reshape(*shape[:dim], shape[dim] * shape[dim + 1], *shape[dim + 2 :])


def collect(array, axis, dim):
    blocks = from_everyone(array, axis)
    return laid_out(blocks, dim)


def split_up(array, dim, peers):
    shape = array.shape
    blocks = array.reshape(*shape[:dim], peers, shape[dim] // peers, *shape[dim + 1 :])
    return jnp.moveaxis(blocks, dim, 0)


def sum_at_owner(array, axis, dim):
    peers = lax.axis_size(axis)
    blocks = lax.all_to_all(split_up(array, dim, peers), axis, 0, 0, tiled=True)
    return jnp.sum(blocks, axis=0)


def padded_2(array, sides, width):
    edges = {}
    for axis, dim in sides:
        peers, length = (lax.axis_size(axis), array.shape[dim])
        up = [(i, (i + 1) % peers) for i in range(peers - 1)]
        last = lax.slice_in_dim(array, length - width, length, axis=dim)
        leading = lax.slice_in_dim(array, 0, width, axis=dim)
        edges[dim] = (
            lax.ppermute(last, axis, up),
            lax.ppermute(leading, axis, [(b, a) for a, b in up]),
        )
    done = []
    for _, dim in sides:
        low, high = edges[dim]
        around = [(width, width) if d in done else (0, 0) for d in range(array.ndim)]
        array = jnp.concatenate([jnp.pad(low, around), array, jnp.pad(high, around)], axis=dim)
        done.append(dim)
    return array


def from_behind(block, axis, distance):
    devices = range(lax.axis_size(axis))
    route = [(i - distance, i) for i in devices if i - distance in devices]
    return lax.ppermute(block, axis, route)


def harmonic(near_value, far_value):
    summed = near_value + far_value
    divisor = jnp.where(summed > 0, summed, 1.0)
    return 2.0 * near_value * far_value / divisor


def neighbours(padded, row_count):
    widened = jnp.pad(padded, ((0, 0), (1, 1)))
    return [
        widened[0:row_count, 1:-1],
        widened[2 : row_count + 2, 1:-1],
        widened[1 : row_count + 1, 0:-2],
        widened[1 : row_count + 1, 2:],
    ]


def prepare(summed_pad, storage, source, pressure_old):
    row_count = storage.shape[0]
    trans_pad = summed_pad[0]
    buoy_pad = summed_pad[1]
    drive_pad = buoyancy_scale * summed_pad[2]
    trans_faces = [
        harmonic(trans_pad[1 : row_count + 1], neighbour)
        for neighbour in neighbours(trans_pad, row_count)
    ]
    buoy_faces = [
        harmonic(buoy_pad[1 : row_count + 1], neighbour)
        for neighbour in neighbours(buoy_pad, row_count)
    ]
    drive_centre = drive_pad[1 : row_count + 1]
    gravity_drive = sum(
        (
            face_coef * (neighbour - drive_centre)
            for face_coef, neighbour in zip(buoy_faces, neighbours(drive_pad, row_count))
        )
    )
    right_hand = storage * pressure_old + source + gravity_drive
    diagonal = storage + trans_faces[0] + trans_faces[1] + trans_faces[2] + trans_faces[3]
    return (trans_faces, right_hand, diagonal)


def relax(trans_faces, right_hand, diagonal, padded):
    row_count = right_hand.shape[0]
    inflow = sum(
        (
            face_coef * neighbour
            for face_coef, neighbour in zip(trans_faces, neighbours(padded, row_count))
        )
    )
    return (right_hand + inflow) / diagonal


def column_depths(every_thick, layer_count, caprock, plume, limit):
    block_count = every_thick.shape[0] // layer_count

    def add_block(block, carry):
        height, above = carry
        first = block * layer_count
        thick_block = lax.dynamic_slice_in_dim(every_thick, first, layer_count, 0)[:, None, None]
        depth = first + lax.broadcasted_iota(jnp.int32, (layer_count, 1, 1), 0)
        gas = (depth >= caprock[None]) & (depth < plume[None])
        height = height + jnp.sum(jnp.where(gas, thick_block, 0.0), axis=0)
        above = above + jnp.sum(jnp.where(gas & (depth < limit), thick_block, 0.0), axis=0)
        return (height, above)

    zeros = jnp.zeros(caprock.shape, jnp.float32)
    return lax.fori_loop(0, block_count, add_block, (zeros, zeros))


def local(permeability, mobility, thickness, caprock, plume, storage, source, pressure_old):
    layer_count = permeability.shape[0]
    layer_index = lax.axis_index("layer")
    layers = layer_index * layer_count + lax.broadcasted_iota(jnp.int32, permeability.shape, 0)
    open_cell = layers >= caprock[None]
    gas_cell = open_cell & (layers < plume[None])
    layer_thick = thickness[:, None, None]
    conduct = jnp.where(open_cell, permeability * mobility * layer_thick, 0.0)
    every_thick = collect(thickness, "layer", 0)
    limit = layer_index * layer_count
    gas_height, gas_above = column_depths(every_thick, layer_count, caprock, plume, limit)
    column_parts = jnp.stack(
        [jnp.sum(conduct, axis=0), jnp.sum(jnp.where(gas_cell, conduct, 0.0), axis=0)]
    )
    slab = sum_at_owner(column_parts, "layer", 1)
    row_count = slab.shape[1]
    slab_start = layer_index * row_count
    slab = jnp.concatenate(
        [slab, lax.dynamic_slice_in_dim(gas_height, slab_start, row_count, 0)[None]], axis=0
    )
    slab_storage = lax.dynamic_slice_in_dim(storage, slab_start, row_count, 0)
    slab_source = lax.dynamic_slice_in_dim(source, slab_start, row_count, 0)
    slab_old = lax.dynamic_slice_in_dim(pressure_old, slab_start, row_count, 0)
    padded = padded_2(slab, ((("area", "layer"), 1),), 1)
    trans_faces, right_hand, diagonal = prepare(padded, slab_storage, slab_source, slab_old)
    pressure = slab_old
    for sweep_index in range(SWEEPS):
        pressure_pad = padded_2(pressure, ((("area", "layer"), 0),), 1)
        pressure = relax(trans_faces, right_hand, diagonal, pressure_pad)
    pressure = collect(pressure, "layer", 0)
    layer_mass = layer_thick * jnp.where(gas_cell, gas_density, brine_density)
    depth_all = lax.broadcasted_iota(jnp.int32, every_thick.shape, 0)
    thick_over = jnp.sum(jnp.where(depth_all < limit, every_thick, 0.0))
    mass_over = thick_over - (brine_density - gas_density) * gas_above
    hydro_head = mass_over[None] + jnp.cumsum(layer_mass, axis=0) - 0.5 * layer_mass
    cell_pressure = pressure[None] + gravity_scale * hydro_head
    edge_rows = jnp.stack([conduct[:, 0, :], cell_pressure[:, 0, :]])
    beyond = from_behind(edge_rows, "area", -1)
    next_conduct = jnp.concatenate([conduct[:, 1:, :], beyond[0][:, None, :]], axis=1)
    next_pressure = jnp.concatenate([cell_pressure[:, 1:, :], beyond[1][:, None, :]], axis=1)
    flux_rows = harmonic(conduct, next_conduct) * (cell_pressure - next_pressure)
    side_conduct = jnp.pad(conduct[:, :, 1:], ((0, 0), (0, 0), (0, 1)))
    side_pressure = jnp.pad(cell_pressure[:, :, 1:], ((0, 0), (0, 0), (0, 1)))
    flux_cols = harmonic(conduct, side_conduct) * (cell_pressure - side_pressure)
    return (cell_pressure, flux_rows, flux_cols)


def solution(mesh):
    in_specs = (
        P("layer", "area", None),
        P("layer", "area", None),
        P("layer"),
        P("area", None),
        P("area", None),
        P("area", None),
        P("area", None),
        P("area", None),
    )
    out_specs = (P("layer", "area", None), P("layer", "area", None), P("layer", "area", None))
    return jax.shard_map(local, mesh=mesh, in_specs=in_specs, out_specs=out_specs, check_vma=False)
```

profile of v0, /device:TPU:0, one launch (start us, length us, event | category | flops | bytes accessed | tf_op | source)
XLA Modules:
  0.0 147.4 jit_solution(15477999659627336950)
XLA Ops:
  0.6 1.2 broadcast_in_dim.85
  1.9 7.7 %all-to-all-start.1 = ((f32[8,1,4]{2,1,0:T(1,128)}), f32[8,1,4]{2,1,0:T(1,128)S(1)}, u32[]{:S(2)}, u32[]{:S(2)}) async-start(f32[8,1,4]{2,1,0:T(1,128)} %broadcast_in_dim.85), calls=%async_computation.1 | async-start | bytes 8192 | tf_op jit(solution)/shard_map/all_to_all | solution.py:17
  9.6 1.3 constant_dynamic-slice_fusion.1
  10.9 3.9 %collective-permute-start.2 = (f32[1,512]{1,0:T(1,128)}, f32[1,512]{1,0:T(1,128)S(1)}, u32[]{:S(2)}, u32[]{:S(2)}) collective-permute-start(f32[1,512]{1,0:T(1,128)} %get-tuple-element.181), channel_id=1, source_target_pairs={{0,1},{1,2},{2,3},{3,4},{4,5},{5,6},{6,7},{7,8},{8,9},{9,10},{10,1... | collective-permute-start | bytes 6152 | tf_op jit(solution)/shard_map/ppermute | solution.py:51
  14.9 1.3 collective-permute-start.3
  16.2 1.6 %constant_dynamic-slice_fusion.2 = f32[64,512]{1,0:T(8,128)} fusion(f32[512,512]{1,0:T(8,128)} %param.17, s32[]{:T(128)S(6)} %select_n.75), kind=kLoop, calls=%fused_computation.138 | loop fusion | bytes 262148 | tf_op jit(solution)/shard_map/dynamic_slice | solution.py:160
  17.7 7.8 %fusion.59 = (f32[512,512]{1,0:T(8,128)S(1)}, f32[512,512]{1,0:T(8,128)S(1)}, f32[4,512,512]{2,1,0:T(8,128)}) fusion(s32[512,512]{1,0:T(8,128)} %param.14, s32[512,512]{1,0:T(8,128)} %param.13, s32[4]{0:T(128)S(1)} %iota_add_fusion.1, f32[4]{0:T(128)} %param.12, f32[4,512,512]{2,1,0:T(8,128)} %param.10, f32[4,512,512]{2,1,0:T(8,128)} %param.11), kind=kLoop, calls=%fused_computation.143 | loop fusion | flops 8912896 | bytes 16777248 | tf_op jit(solution)/shard_map/reduce_sum | solution.py:150
  25.5 1.5 %maximum_bitcast_fusion = f32[8,2,64,512]{3,2,1,0:T(8,128)} fusion(f32[1,8,64,512]{3,2,0,1:T(8,128)S(1)} %bitcast.94, f32[1,8,64,512]{3,2,0,1:T(8,128)S(1)} %bitcast.93), kind=kLoop, calls=%fused_computation.21 | loop fusion | flops 524288 | bytes 4194304 | tf_op jit(solution)/shard_map/transpose | solution.py:34
  27.0 9.0 %all-to-all-start = ((f32[8,2,64,512]{3,2,1,0:T(8,128)}), f32[8,2,64,512]{3,2,1,0:T(8,128)}, u32[]{:S(2)}, u32[]{:S(2)}) async-start(f32[8,2,64,512]{3,2,1,0:T(8,128)} %maximum_bitcast_fusion), calls=%async_computation | async-start | bytes 4194304 | tf_op jit(solution)/shard_map/all_to_all | solution.py:39
  37.3 25.2 %while.16 = (s32[]{:T(128)}, f32[512,512]{1,0:T(8,128)}, f32[512,512]{1,0:T(8,128)S(1)}, s32[512,512]{1,0:T(8,128)S(1)}, s32[512,512]{1,0:T(8,128)S(1)}, /*index...) while((s32[]{:T(128)}, f32[512,512]{1,0:T(8,128)}, ...), condition=%wide.region_6.7_spmd.clone, body=%wide.region_3.0_spmd.clone.sunk | while | flops 8912915 | bytes 18874700 | solution.py:135
  37.4 1.3 select_reduce_fusion.4
  39.5 1.0 copy-done.5
  40.5 1.3 select_reduce_fusion.4
  42.6 1.0 copy-done.5
  43.7 1.3 select_reduce_fusion.4
  45.8 1.0 copy-done.5
  46.8 1.3 select_reduce_fusion.4
  48.9 1.0 copy-done.5
  50.0 1.3 select_reduce_fusion.4
  52.1 1.0 copy-done.5
  53.1 1.3 select_reduce_fusion.4
  56.3 1.3 select_reduce_fusion.4
  59.4 1.3 select_reduce_fusion.4
  63.4 1.2 all-to-all-done
  64.6 1.8 %reduce_sum.64 = f32[2,64,512]{2,1,0:T(8,128)S(1)} reduce(f32[8,2,64,512]{3,2,1,0:T(8,128)} %all-to-all-done, f32[]{:T(128)} %constant.63.clone.1), dimensions={0}, to_apply=%region_2.3 | reduce | flops 458752 | bytes 2359300 | tf_op jit(solution)/shard_map/reduce_sum | solution.py:40
  66.5 2.8 %collective-permute-start = (f32[3,1,512]{2,1,0:T(1,128)S(1)}, f32[3,1,512]{2,1,0:T(1,128)S(1)}, u32[]{:S(2)}, u32[]{:S(2)}) collective-permute-start(f32[3,1,512]{2,1,0:T(1,128)S(1)} %get-tuple-element.187), channel_id=1, source_target_pairs={{0,1},{1,2},{2,3},{3,4},{4,5},{5,6},{6,7},{7,8},{8,9},{9,10},{10,1... | collective-permute-start | bytes 18440 | tf_op jit(solution)/shard_map/ppermute | solution.py:51
  69.2 1.3 collective-permute-start.1
  70.5 1.0 select_maximum_fusion.4
  71.6 3.2 %collective-permute-done.1 = f32[3,1,512]{2,1,0:T(1,128)S(1)} collective-permute-done((f32[3,1,512]{2,1,0:T(1,128)S(1)}, f32[3,1,512]{2,1,0:T(1,128)S(1)}, u32[]{:S(2)}, u32[]{:S(2)}) %collective-permute-start.1) | collective-permute-done | bytes 6176 | tf_op jit(solution)/shard_map/ppermute | solution.py:52
  74.9 1.8 %fusion.46 = (f32[64,512]{1,0:T(8,128)S(1)}, f32[64,512]{1,0:T(8,128)S(1)}, f32[64,512]{1,0:T(8,128)S(1)}, f32[64,512]{1,0:T(8,128)S(1)}) fusion(f32[66,514]{1,0:T(8,128)S(1)} %select_maximum_fusion.4, f32[1,512]{1,0:T(1,128)S(1)} %collective-permute-done.3, f32[64,512]{1,0:T(8,128)} %constant_dynamic-slice_fusion.2, ...), kind=kLoop, calls=%fused_computation.99 | loop fusion | flops 2588672 | bytes 2818052 | tf_op jit(solution)/shard_map/div | solution.py:118
  76.6 3.3 %collective-permute-start.4 = (f32[1,512]{1,0:T(1,128)S(1)}, f32[1,512]{1,0:T(1,128)S(1)}, u32[]{:S(2)}, u32[]{:S(2)}) collective-permute-start(f32[1,512]{1,0:T(1,128)S(1)} %get-tuple-element.191), channel_id=1, source_target_pairs={{0,1},{1,2},{2,3},{3,4},{4,5},{5,6},{6,7},{7,8},{8,9},{9,10},{10,1... | collective-permute-start | bytes 6152 | tf_op jit(solution)/shard_map/ppermute | solution.py:51
  80.0 1.3 collective-permute-start.5
  81.3 4.3 %collective-permute-done.5 = f32[1,512]{1,0:T(1,128)S(1)} collective-permute-done((f32[1,512]{1,0:T(1,128)S(1)}, f32[1,512]{1,0:T(1,128)S(1)}, u32[]{:S(2)}, u32[]{:S(2)}) %collective-permute-start.5) | collective-permute-done | bytes 2080 | tf_op jit(solution)/shard_map/ppermute | solution.py:52
  85.7 1.1 fusion.39
  86.9 7.5 %collective-permute-start.6 = (f32[1,512]{1,0:T(1,128)S(1)}, f32[1,512]{1,0:T(1,128)S(1)}, u32[]{:S(2)}, u32[]{:S(2)}) collective-permute-start(f32[1,512]{1,0:T(1,128)S(1)} %get-tuple-element.189), channel_id=1, source_target_pairs={{0,1},{1,2},{2,3},{3,4},{4,5},{5,6},{6,7},{7,8},{8,9},{9,10},{10,1... | collective-permute-start | bytes 6152 | tf_op jit(solution)/shard_map/ppermute | solution.py:51
  94.4 1.3 collective-permute-start.7
  95.7 4.2 %collective-permute-done.7 = f32[1,512]{1,0:T(1,128)S(1)} collective-permute-done((f32[1,512]{1,0:T(1,128)S(1)}, f32[1,512]{1,0:T(1,128)S(1)}, u32[]{:S(2)}, u32[]{:S(2)}) %collective-permute-start.7) | collective-permute-done | bytes 2080 | tf_op jit(solution)/shard_map/ppermute | solution.py:52
  100.0 1.1 fusion.32
  101.2 1.1 broadcast_in_dim.88
  102.3 9.1 %all-to-all-start.2 = ((f32[8,64,512]{2,1,0:T(8,128)}), f32[8,64,512]{2,1,0:T(8,128)}, u32[]{:S(2)}, u32[]{:S(2)}) async-start(f32[8,64,512]{2,1,0:T(8,128)} %broadcast_in_dim.88), calls=%async_computation.2 | async-start | bytes 2097152 | tf_op jit(solution)/shard_map/all_to_all | solution.py:17
  113.0 1.7 %multiply_subtract_fusion = f32[512,512]{1,0:T(8,128)} fusion(f32[512,512]{1,0:T(8,128)S(1)} %get-tuple-element.129, f32[]{:T(128)} %fusion.55), kind=kLoop, calls=%fused_computation.28 | loop fusion | flops 524288 | bytes 2097156 | tf_op jit(solution)/shard_map/sub | solution.py:171
  114.7 15.0 %all-to-all-done.2 = f32[8,64,512]{2,1,0:T(8,128)} async-done(((f32[8,64,512]{2,1,0:T(8,128)}), f32[8,64,512]{2,1,0:T(8,128)}, u32[]{:S(2)}, u32[]{:S(2)}) %all-to-all-start.2) | async-done | bytes 1048608 | tf_op jit(solution)/shard_map/all_to_all | solution.py:17
  129.7 3.9 %multiply_add_fusion = f32[4,512,512]{2,1,0:T(8,128)S(1)} fusion(f32[512,512]{1,0:T(8,128)} %multiply_subtract_fusion, f32[512,512]{1,0:T(8,128)} %bitcast.16, s32[512,512]{1,0:T(8,128)S(1)} %get-tuple-element.280, f32[4]{0:T(128)S(1)} %copy-done.6, s32[512,512]{1,0:T(8,128)S(1)} %get-tuple-element.279, s32[4]{0:T(128)S(1)} %iota_add_fusion.1), kind=kOutput, calls=%fused_computation.17 | output fusion | flops 18874368 | bytes 8388640 | tf_op jit(solution)/shard_map/jit(cumsum)/reduce_window_sum | solution.py:172
  133.7 1.5 collective-permute-start.8
  135.8 1.1 slice.282
  137.0 1.1 slice.283
  138.1 2.5 %slice.280 = f32[4,511,512]{2,1,0:T(8,128)} slice(f32[4,512,512]{2,1,0:T(8,128)S(1)} %multiply_add_fusion), slice={[0:4], [1:512], [0:512]} | slice | bytes 8372224 | tf_op jit(solution)/shard_map/slice | solution.py:177
  140.6 6.8 %fusion.3 = (f32[4,512,512]{2,1,0:T(8,128)}, f32[4,512,512]{2,1,0:T(8,128)}) fusion(f32[4,512,512]{2,1,0:T(8,128)S(1)} %multiply_add_fusion, f32[4,512,511]{2,1,0:T(8,128)S(1)} %slice.283, f32[4,512,512]{2,1,0:T(8,128)S(1)} %copy-done.1, f32[4,512,511]{2,1,0:T(8,128)S(1)} %slice.282, f32[4,1,512]{2,1,0:T(1,128)S(1)} %get-tuple-element.194, ...), kind=kLoop, calls=%fused_computation.14 | loop fusion | flops 17825792 | bytes 33538048 | tf_op jit(solution)/shard_map/mul | solution.py:181
  (97 shorter events, 14.2 us)
Async XLA Ops:
  1.9 25.1 %all-to-all-start.1 = ((f32[8,1,4]{2,1,0:T(1,128)}), f32[8,1,4]{2,1,0:T(1,128)S(1)}, u32[]{:S(2)}, u32[]{:S(2)}) async-start(f32[8,1,4]{2,1,0:T(1,128)} %broadcast_in_dim.85), calls=%async_computation.1 | async-start | bytes 8192 | tf_op jit(solution)/shard_map/all_to_all | solution.py:17
  10.9 59.6 %collective-permute-start.2 = (f32[1,512]{1,0:T(1,128)}, f32[1,512]{1,0:T(1,128)S(1)}, u32[]{:S(2)}, u32[]{:S(2)}) collective-permute-start(f32[1,512]{1,0:T(1,128)} %get-tuple-element.181), channel_id=1, source_target_pairs={{0,1},{1,2},{2,3},{3,4},{4,5},{5,6},{6,7},{7,8},{8,9},{9,10},{10,1... | collective-permute-start | bytes 6152 | tf_op jit(solution)/shard_map/ppermute | solution.py:51
  14.9 55.7 %collective-permute-start.3 = (f32[1,512]{1,0:T(1,128)}, f32[1,512]{1,0:T(1,128)S(1)}, u32[]{:S(2)}, u32[]{:S(2)}) collective-permute-start(f32[1,512]{1,0:T(1,128)} %get-tuple-element.182), channel_id=1, source_target_pairs={{1,0},{2,1},{3,2},{4,3},{5,4},{6,5},{7,6},{8,7},{9,8},{10,9},{11,1... | collective-permute-start | bytes 6152 | tf_op jit(solution)/shard_map/ppermute | solution.py:52
  25.5 11.8 %copy-start.2 = (s32[512,512]{1,0:T(8,128)S(1)}, s32[512,512]{1,0:T(8,128)}, u32[]{:S(2)}) copy-start(s32[512,512]{1,0:T(8,128)} %param.13) | copy-start | bytes 3145732
  25.5 11.8 %copy-start.3 = (s32[512,512]{1,0:T(8,128)S(1)}, s32[512,512]{1,0:T(8,128)}, u32[]{:S(2)}) copy-start(s32[512,512]{1,0:T(8,128)} %param.14) | copy-start | bytes 3145732
  27.0 37.6 %all-to-all-start = ((f32[8,2,64,512]{3,2,1,0:T(8,128)}), f32[8,2,64,512]{3,2,1,0:T(8,128)}, u32[]{:S(2)}, u32[]{:S(2)}) async-start(f32[8,2,64,512]{3,2,1,0:T(8,128)} %maximum_bitcast_fusion), calls=%async_computation | async-start | bytes 4194304 | tf_op jit(solution)/shard_map/all_to_all | solution.py:39
  37.3 1.4 copy-start.4
  39.5 1.0 copy-start.5
  40.5 1.4 copy-start.4
  42.6 1.0 copy-start.5
  43.6 1.4 copy-start.4
  45.8 1.0 copy-start.5
  46.8 1.4 copy-start.4
  48.9 1.0 copy-start.5
  49.9 1.4 copy-start.4
  52.1 1.0 copy-start.5
  53.0 1.4 copy-start.4
  55.2 1.0 copy-start.5
  56.2 1.4 copy-start.4
  58.4 1.0 copy-start.5
  59.3 1.4 copy-start.4
  61.5 1.0 copy-start.5
  66.5 5.1 %collective-permute-start = (f32[3,1,512]{2,1,0:T(1,128)S(1)}, f32[3,1,512]{2,1,0:T(1,128)S(1)}, u32[]{:S(2)}, u32[]{:S(2)}) collective-permute-start(f32[3,1,512]{2,1,0:T(1,128)S(1)} %get-tuple-element.187), channel_id=1, source_target_pairs={{0,1},{1,2},{2,3},{3,4},{4,5},{5,6},{6,7},{7,8},{8,9},{9,10},{10,1... | collective-permute-start | bytes 18440 | tf_op jit(solution)/shard_map/ppermute | solution.py:51
  69.2 5.5 %collective-permute-start.1 = (f32[3,1,512]{2,1,0:T(1,128)S(1)}, f32[3,1,512]{2,1,0:T(1,128)S(1)}, u32[]{:S(2)}, u32[]{:S(2)}) collective-permute-start(f32[3,1,512]{2,1,0:T(1,128)S(1)} %get-tuple-element.188), channel_id=1, source_target_pairs={{1,0},{2,1},{3,2},{4,3},{5,4},{6,5},{7,6},{8,7},{9,8},{10,9},{11,1... | collective-permute-start | bytes 18440 | tf_op jit(solution)/shard_map/ppermute | solution.py:52
  76.6 4.6 %collective-permute-start.4 = (f32[1,512]{1,0:T(1,128)S(1)}, f32[1,512]{1,0:T(1,128)S(1)}, u32[]{:S(2)}, u32[]{:S(2)}) collective-permute-start(f32[1,512]{1,0:T(1,128)S(1)} %get-tuple-element.191), channel_id=1, source_target_pairs={{0,1},{1,2},{2,3},{3,4},{4,5},{5,6},{6,7},{7,8},{8,9},{9,10},{10,1... | collective-permute-start | bytes 6152 | tf_op jit(solution)/shard_map/ppermute | solution.py:51
  80.0 5.6 %collective-permute-start.5 = (f32[1,512]{1,0:T(1,128)S(1)}, f32[1,512]{1,0:T(1,128)S(1)}, u32[]{:S(2)}, u32[]{:S(2)}) collective-permute-start(f32[1,512]{1,0:T(1,128)S(1)} %get-tuple-element.192), channel_id=1, source_target_pairs={{1,0},{2,1},{3,2},{4,3},{5,4},{6,5},{7,6},{8,7},{9,8},{10,9},{11,1... | collective-permute-start | bytes 6152 | tf_op jit(solution)/shard_map/ppermute | solution.py:52
  85.7 44.0 %copy-start.6 = (f32[4]{0:T(128)S(1)}, f32[4]{0:T(128)}, u32[]{:S(2)}) copy-start(f32[4]{0:T(128)} %param.12) | copy-start | bytes 52
  86.9 8.8 %collective-permute-start.6 = (f32[1,512]{1,0:T(1,128)S(1)}, f32[1,512]{1,0:T(1,128)S(1)}, u32[]{:S(2)}, u32[]{:S(2)}) collective-permute-start(f32[1,512]{1,0:T(1,128)S(1)} %get-tuple-element.189), channel_id=1, source_target_pairs={{0,1},{1,2},{2,3},{3,4},{4,5},{5,6},{6,7},{7,8},{8,9},{9,10},{10,1... | collective-permute-start | bytes 6152 | tf_op jit(solution)/shard_map/ppermute | solution.py:51
  94.4 5.5 %collective-permute-start.7 = (f32[1,512]{1,0:T(1,128)S(1)}, f32[1,512]{1,0:T(1,128)S(1)}, u32[]{:S(2)}, u32[]{:S(2)}) collective-permute-start(f32[1,512]{1,0:T(1,128)S(1)} %get-tuple-element.190), channel_id=1, source_target_pairs={{1,0},{2,1},{3,2},{4,3},{5,4},{6,5},{7,6},{8,7},{9,8},{10,9},{11,1... | collective-permute-start | bytes 6152 | tf_op jit(solution)/shard_map/ppermute | solution.py:52
  102.3 27.5 %all-to-all-start.2 = ((f32[8,64,512]{2,1,0:T(8,128)}), f32[8,64,512]{2,1,0:T(8,128)}, u32[]{:S(2)}, u32[]{:S(2)}) async-start(f32[8,64,512]{2,1,0:T(8,128)} %broadcast_in_dim.88), calls=%async_computation.2 | async-start | bytes 2097152 | tf_op jit(solution)/shard_map/all_to_all | solution.py:17
  129.7 5.4 %copy-start.1 = (f32[4,512,512]{2,1,0:T(8,128)S(1)}, f32[4,512,512]{2,1,0:T(8,128)}, u32[]{:S(2)}) copy-start(f32[4,512,512]{2,1,0:T(8,128)} %get-tuple-element.176) | copy-start | bytes 12582916
  133.6 7.0 %copy-start = (f32[4,512,512]{2,1,0:T(8,128)}, f32[4,512,512]{2,1,0:T(8,128)S(1)}, u32[]{:S(2)}) copy-start(f32[4,512,512]{2,1,0:T(8,128)S(1)} %multiply_add_fusion) | copy-start | bytes 12582916
  133.7 6.9 %collective-permute-start.8 = (f32[2,4,512]{2,0,1:T(2,128)S(1)}, f32[2,4,512]{2,0,1:T(2,128)S(1)}, u32[]{:S(2)}, u32[]{:S(2)}) collective-permute-start(f32[2,4,512]{2,0,1:T(2,128)S(1)} %pad_maximum_fusion.12), channel_id=1, source_target_pairs={{8,0},{16,8},{24,16},{32,24},{40,32},{48,40},{56,48},{64,56},{72,6... | collective-permute-start | bytes 49160 | tf_op jit(solution)/shard_map/ppermute | solution.py:66
where the time goes:
time: 150 us; the launch traced here: 147 us
  starting transfers between devices  50.1 us (33%)
  other arithmetic  46.8 us (31%)
  waiting for transfers between devices  27.9 us (19%)
  local copies, waits for them, and re-layouts  21.5 us (14%)
    ppermute x4, starting transfers between devices, padded_2(): lax.ppermute(last, axis, up)  17.5 us
    all_to_all x2, starting transfers between devices, from_everyone(): return lax.all_to_all(copies, axis, split_axis=0, concat_axis=0, tiled=True)  16.8 us
    all_to_all x2, waiting for transfers between devices, from_everyone(): return lax.all_to_all(copies, axis, split_axis=0, concat_axis=0, tiled=True)  15.1 us
    ppermute x4, waiting for transfers between devices, padded_2(): lax.ppermute(leading, axis, [(b, a) for a, b in up])  11.6 us
    reduce_sum x8, other arithmetic, add_block(): jnp.sum(jnp.where(gas & (depth < limit), thick_block, 0.0), axis=0)  10.7 us
    all_to_all x1, starting transfers between devices, sum_at_owner(): blocks = lax.all_to_all(split_up(array, dim, peers), axis, 0, 0, tiled=True)  9.04 us
    reduce_sum x1, other arithmetic, local(): jnp.sum(conduct, axis=0)  7.76 us
    while x32, local copies, waits for them, and re-layouts  7.75 us
  transfers between devices with their start and end apart: 12, of which 5 were waited for; matrix products, arithmetic and copies ran while one was open for 29% of the time, Pallas kernels for 0%

commit v1 on v0

v1 whole, which is shorter than its diff:
```python
import functools

import jax
import jax.numpy as jnp
from jax import lax
from jax.experimental import pallas as pl
from jax.experimental.pallas import tpu as pltpu
from jax.sharding import PartitionSpec as P

SWEEPS = 3
buoyancy_scale = 0.3
gravity_scale = 0.05
gas_density = 0.7
brine_density = 1.0

LAYERS = 4
ROWS = 512
COLS = 512
SLAB = 64
HALO = 8
WIDE = SLAB + 2 * HALO
MESH = pl.DeviceIdType.MESH

ORDERS = ((0, 1, 2), (1, 2, 0), (2, 0, 1))
PART_START = (0, 24, 48)
PART_ROWS = (24, 24, 16)
FLIPS = ((1, 1, 1), (1, 1, 0), (0, 1, 1), (1, 0, 1), (1, 0, 0), (0, 1, 0), (0, 0, 1), (0, 0, 0))
OTHERS = FLIPS[:-1]


def harmonic(near_value, far_value):
    summed = near_value + far_value
    divisor = jnp.where(summed > 0, summed, 1.0)
    return 2.0 * near_value * far_value / divisor


def flip_of(*dims):
    return tuple(1 if d in dims else 0 for d in range(3))


class Place:
    def __init__(self):
        self.area = lax.axis_index("area")
        self.layer = lax.axis_index("layer")
        self.areas = lax.axis_size("area")
        x = self.layer % 4
        second = x // 2
        first = (x % 2) + second - 2 * (x % 2) * second
        self.code = (first, second, self.layer // 4)
        self.parity = self.area % 2
        self.slab = self.slab_of((0, 0, 0))

    def flipped(self, flip):
        return tuple((1 - c) if f else c for c, f in zip(self.code, flip))

    def layer_of(self, flip):
        first, second, half = self.flipped(flip)
        x = 2 * second + first + second - 2 * first * second
        return half * 4 + x

    def slab_of(self, flip):
        first, second, half = self.flipped(flip)
        x = 2 * second + first + second - 2 * first * second
        order = x + half * (7 - 2 * x)
        return order + self.parity * (7 - 2 * order)

    def layer_of_slab(self, slab):
        order = slab + self.parity * (7 - 2 * slab)
        return order + (order // 4) * (11 - 2 * order)

    def rows(self, flip, start, count):
        return pl.ds(pl.multiple_of(self.slab_of(flip) * SLAB + start, 8), count)


def gather_kernel(
    perm, mob, thick, cap, plu, sto, src, old,
    hh, hr, gr, hc, gc, pf,
    permv, mobv, cond, capv, pluv, tb, r1a, r1b, r1c, r2a, r2b, r2c, r3a, r3b, r3c,
    wide, edge_i, edge_f, thick_s, thick_all, table, gas, t_row, t_col, right_hand, inverse,
    in_sem, edge_sem, thick_sem, rs_send, rs_recv, ag_send, ag_recv, th_send, th_recv,
    halo_send, halo_recv, input_send, input_recv, row_send, row_recv, last_send, last_recv,
):
    here = Place()
    area, layer = here.area, here.layer
    r1, r2, r3 = (r1a, r1b, r1c), (r2a, r2b, r2c), (r3a, r3b, r3c)
    waits = []
    is_first = here.slab == 0
    is_last = here.slab == 7

    def peer(flip):
        return (area, here.layer_of(flip))

    loads = []
    thick_copy = pltpu.make_async_copy(thick, thick_s, thick_sem.at[0])
    thick_copy.start()
    for n, flip in enumerate(FLIPS):
        rows = here.rows(flip, 0, SLAB)
        group = [
            pltpu.make_async_copy(cap.at[rows], capv.at[rows], in_sem.at[n, 0]),
            pltpu.make_async_copy(plu.at[rows], pluv.at[rows], in_sem.at[n, 1]),
            pltpu.make_async_copy(perm.at[:, rows], permv.at[:, rows], in_sem.at[n, 2]),
            pltpu.make_async_copy(mob.at[:, rows], mobv.at[:, rows], in_sem.at[n, 3]),
        ]
        for copy in group:
            copy.start()
        loads.append(group)

    barrier = pltpu.get_barrier_semaphore()
    for flip in OTHERS:
        pl.semaphore_signal(barrier, inc=1, device_id=peer(flip), device_id_type=MESH)
    for step in (1, here.areas - 1):
        pl.semaphore_signal(
            barrier, inc=1, device_id=((area + step) % here.areas, layer), device_id_type=MESH
        )

    base = here.slab * SLAB
    sources = (cap, plu, sto, src, old)
    targets = (edge_i.at[0], edge_i.at[1], edge_f.at[0], edge_f.at[1], edge_f.at[2])

    def edge_copies(sem_row, first_row, count, at):
        rows = pl.ds(pl.multiple_of(base + first_row, 8), count)
        return [
            pltpu.make_async_copy(s.at[rows], t.at[pl.ds(at, count)], edge_sem.at[sem_row, n])
            for n, (s, t) in enumerate(zip(sources, targets))
        ]

    mid_copies = edge_copies(0, 0, SLAB, HALO)
    for copy in mid_copies:
        copy.start()

    @pl.when(here.slab > 0)
    def _():
        for copy in edge_copies(1, -HALO, HALO, 0):
            copy.start()

    @pl.when(here.slab < 7)
    def _():
        for copy in edge_copies(2, SLAB, HALO, HALO + SLAB):
            copy.start()

    thick_copy.wait()
    sublane = lax.broadcasted_iota(jnp.int32, (8, 128), 0)
    tile = jnp.zeros((8, 128), jnp.float32)
    for k in range(LAYERS):
        tile = jnp.where(sublane == k, thick_s[k], tile)
    thick_all[layer] = tile

    def input_sends():
        up = [
            pltpu.make_async_remote_copy(
                s.at[pl.ds(0, HALO)], t.at[pl.ds(HALO + SLAB, HALO)],
                input_send.at[0, n], input_recv.at[0, n],
                device_id=(area - 1, layer), device_id_type=MESH,
            )
            for n, (s, t) in enumerate(zip(sources, targets))
        ]
        down = [
            pltpu.make_async_remote_copy(
                s.at[pl.ds(ROWS - HALO, HALO)], t.at[pl.ds(0, HALO)],
                input_send.at[1, n], input_recv.at[1, n],
                device_id=(area + 1, layer), device_id_type=MESH,
            )
            for n, (s, t) in enumerate(zip(sources, targets))
        ]
        return up, down

    to_up, to_down = input_sends()
    crosses_up = is_first & (area > 0)
    crosses_down = is_last & (area < here.areas - 1)
    top_edge = is_first & (area == 0)
    bottom_edge = is_last & (area == here.areas - 1)

    def conduct_slab(n, flip):
        for copy in loads[n]:
            copy.wait()
        start = here.slab_of(flip) * SLAB

        @pl.loop(0, SLAB // 8)
        def _(i):
            rows = pl.ds(pl.multiple_of(start + i * 8, 8), 8)
            top = capv[rows, :]
            bottom = pluv[rows, :]
            trans = None
            for k in range(LAYERS):
                depth = layer * LAYERS + k
                flow = permv[k, rows, :] * mobv[k, rows, :] * thick_s[k]
                flow = jnp.where(depth >= top, flow, 0.0)
                cond[k, rows, :] = flow
                part = jnp.where(depth < bottom, flow, 0.0)
                trans, buoy = (flow, part) if trans is None else (trans + flow, buoy + part)
            tb[0, rows, :] = trans
            tb[1, rows, :] = buoy

    def rs_copy(q, number, rows, buffer, dim):
        return pltpu.make_async_remote_copy(
            tb.at[:, rows], buffer, rs_send.at[q, number], rs_recv.at[q, number],
            device_id=peer(flip_of(dim)), device_id_type=MESH,
        )

    PIECES = ((1, 1), (1, 0), (0, 1), (0, 0))

    def part_rows(q, flip):
        return here.rows(flip, PART_START[q], PART_ROWS[q])

    def first_copy(q, n):
        d1, d2, d3 = ORDERS[q]
        e2, e3 = PIECES[n]
        flip = flip_of(*([d1] + [d2] * e2 + [d3] * e3))
        return flip, rs_copy(q, n, part_rows(q, flip), r1[q].at[n], d1)

    def second_copy(q, n):
        d1, d2, d3 = ORDERS[q]
        flip = flip_of(*([d2] + ([d3] if n == 0 else [])))
        return flip, rs_copy(q, 4 + n, part_rows(q, flip), r2[q].at[n], d2)

    def third_copy(q):
        d1, d2, d3 = ORDERS[q]
        flip = flip_of(d3)
        return flip, rs_copy(q, 6, part_rows(q, flip), r3[q], d3)

    for n, flip in enumerate(FLIPS):
        conduct_slab(n, flip)
        if n == 0:
            pl.semaphore_wait(barrier, 9)
        for q in range(3):
            for m in range(4):
                owner, copy = first_copy(q, m)
                if owner == flip:
                    copy.start()
                    waits.append(copy)
        if n == 0:
            for m, other in enumerate(OTHERS):
                copy = pltpu.make_async_remote_copy(
                    thick_all.at[layer], thick_all.at[layer], th_send.at[m], th_recv.at[m],
                    device_id=peer(other), device_id_type=MESH,
                )
                copy.start()
                waits.append(copy)

            @pl.when(crosses_up)
            def _():
                for copy in to_up:
                    copy.start()

            @pl.when(crosses_down)
            def _():
                for copy in to_down:
                    copy.start()

    def row_copy(n, array):
        return pltpu.make_async_remote_copy(
            array.at[:, pl.ds(0, 8)], array.at[:, pl.ds(ROWS, 8)], row_send.at[n], row_recv.at[n],
            device_id=(area - 1, layer), device_id_type=MESH,
        )

    @pl.when(area > 0)
    def _():
        row_copy(0, cond).start()

    for m, other in enumerate(OTHERS):
        pltpu.make_async_remote_copy(
            thick_all.at[layer], thick_all.at[here.layer_of(other)], th_send.at[m], th_recv.at[m],
            device_id=peer(other), device_id_type=MESH,
        ).wait_recv()
    for block in range(8):
        for k in range(LAYERS):
            table[block * LAYERS + k] = jnp.broadcast_to(
                thick_all[block, pl.ds(k, 1), :], (8, 128)
            )

    def across(tile):
        return jnp.concatenate([tile] * (COLS // 128), axis=1)

    over_all = lax.fori_loop(
        0, layer * LAYERS, lambda z, total: total + table[z], jnp.zeros((8, 128), jnp.float32)
    )

    def gas_sum(blocks, top, bottom):
        def add_block(block, total):
            for k in range(LAYERS):
                depth = block * LAYERS + k
                inside = (depth >= top) & (depth < bottom)
                total = total + jnp.where(inside, across(table[depth]), 0.0)
            return total

        return lax.fori_loop(0, blocks, add_block, jnp.zeros(top.shape, jnp.float32))

    def heads(low, high):
        @pl.loop(low, high)
        def _(i):
            rows = pl.ds(pl.multiple_of(i * 8, 8), 8)
            top = capv[rows, :]
            bottom = pluv[rows, :]
            above = across(over_all) - (brine_density - gas_density) * gas_sum(layer, top, bottom)
            for k in range(LAYERS):
                depth = layer * LAYERS + k
                inside = (depth >= top) & (depth < bottom)
                mass = jnp.where(inside, gas_density * thick_s[k], brine_density * thick_s[k])
                hh[k, rows, :] = gravity_scale * (above + 0.5 * mass)
                above = above + mass

    lane_last = lax.broadcasted_iota(jnp.int32, (32, COLS), 1) < COLS - 1

    def faces(low, high):
        @pl.loop(low * LAYERS, high * LAYERS)
        def _(i):
            k = i % LAYERS
            start = pl.multiple_of((i // LAYERS) * 32, 8)
            flow = cond[k, pl.ds(start, 40), :]
            head = hh[k, pl.ds(start, 40), :]
            next_flow = pltpu.roll(flow, 39, 0)[:32]
            next_head = pltpu.roll(head, 39, 0)[:32]
            flow = flow[:32]
            head = head[:32]
            rows = pl.ds(start, 32)
            face = harmonic(flow, next_flow)
            hr[k, rows, :] = face
            gr[k, rows, :] = face * (head - next_head)
            side_flow = jnp.where(lane_last, pltpu.roll(flow, COLS - 1, 1), 0.0)
            side_head = pltpu.roll(head, COLS - 1, 1)
            face = harmonic(flow, side_flow)
            hc[k, rows, :] = face
            gc[k, rows, :] = face * (head - side_head)

    def second(n):
        for q in range(3):
            _, arrived = first_copy(q, n)
            arrived.wait_recv()
            flip, copy = second_copy(q, n)
            rows = part_rows(q, flip)
            tb[:, rows, :] = tb[:, rows, :] + r1[q][n]
            copy.start()
            waits.append(copy)

    second(0)
    heads(0, 32)
    second(1)
    heads(32, 64)

    @pl.when(area > 0)
    def _():
        row_copy(1, hh).start()

    for copy in mid_copies:
        copy.wait()

    @pl.when(here.slab > 0)
    def _():
        for copy in edge_copies(1, -HALO, HALO, 0):
            copy.wait()

    @pl.when(here.slab < 7)
    def _():
        for copy in edge_copies(2, SLAB, HALO, HALO + SLAB):
            copy.wait()

    @pl.when(crosses_up)
    def _():
        for copy in to_down:
            copy.wait_recv()

    @pl.when(crosses_down)
    def _():
        for copy in to_up:
            copy.wait_recv()

    def blank(at):
        rows = pl.ds(at, HALO)
        edge_i[:, rows, :] = jnp.zeros((2, HALO, COLS), jnp.int32)
        edge_f[0, rows, :] = jnp.ones((HALO, COLS), jnp.float32)
        edge_f[1, rows, :] = jnp.zeros((HALO, COLS), jnp.float32)
        edge_f[2, rows, :] = jnp.zeros((HALO, COLS), jnp.float32)
        wide[:, rows, :] = jnp.zeros((2, HALO, COLS), jnp.float32)

    @pl.when(top_edge)
    def _():
        blank(0)

    @pl.when(bottom_edge)
    def _():
        blank(HALO + SLAB)

    @pl.loop(0, WIDE // 8)
    def _(i):
        rows = pl.ds(pl.multiple_of(i * 8, 8), 8)
        gas[rows, :] = buoyancy_scale * gas_sum(8, edge_i[0, rows, :], edge_i[1, rows, :])

    faces(0, 5)

    for q in range(3):
        first_copy(q, 2)[1].wait_recv()
        second_copy(q, 0)[1].wait_recv()
        flip, copy = third_copy(q)
        rows = part_rows(q, flip)
        tb[:, rows, :] = tb[:, rows, :] + (r1[q][2] + r2[q][0])
        copy.start()
        waits.append(copy)

    faces(5, 15)

    @pl.when(area < here.areas - 1)
    def _():
        row_copy(0, cond).wait_recv()
        row_copy(1, hh).wait_recv()

    @pl.when(area == here.areas - 1)
    def _():
        cond[:, pl.ds(ROWS, 8), :] = jnp.zeros((LAYERS, 8, COLS), jnp.float32)
        hh[:, pl.ds(ROWS, 8), :] = jnp.zeros((LAYERS, 8, COLS), jnp.float32)

    faces(15, 16)

    for q in range(3):
        first_copy(q, 3)[1].wait_recv()
        second_copy(q, 1)[1].wait_recv()
        third_copy(q)[1].wait_recv()
        mine = part_rows(q, (0, 0, 0))
        at = pl.ds(HALO + PART_START[q], PART_ROWS[q])
        wide[:, at, :] = tb[:, mine, :] + r1[q][3] + (r2[q][1] + r3[q][...])

    up_area = area - (7 - here.slab) // 7
    up_same = 1 - (7 - here.slab) // 7
    down_area = area + here.slab // 7
    down_same = 1 - here.slab // 7
    up_layer = up_same * here.layer_of_slab(here.slab - up_same) + (1 - up_same) * layer
    down_layer = down_same * here.layer_of_slab(here.slab + down_same) + (1 - down_same) * layer
    halo_up = pltpu.make_async_remote_copy(
        wide.at[:, pl.ds(HALO, HALO)], wide.at[:, pl.ds(HALO + SLAB, HALO)],
        halo_send.at[0], halo_recv.at[0], device_id=(up_area, up_layer), device_id_type=MESH,
    )
    halo_down = pltpu.make_async_remote_copy(
        wide.at[:, pl.ds(SLAB, HALO)], wide.at[:, pl.ds(0, HALO)],
        halo_send.at[1], halo_recv.at[1], device_id=(down_area, down_layer), device_id_type=MESH,
    )
    has_up = area * 8 + here.slab > 0
    has_down = area * 8 + here.slab < here.areas * 8 - 1

    @pl.when(has_up)
    def _():
        halo_up.start()

    @pl.when(has_down)
    def _():
        halo_down.start()

    @pl.when(has_up)
    def _():
        halo_down.wait_recv()

    @pl.when(has_down)
    def _():
        halo_up.wait_recv()

    lane = lax.broadcasted_iota(jnp.int32, (WIDE, COLS), 1)

    def after(x):
        return pltpu.roll(x, WIDE - 1, 0)

    def before(x):
        return pltpu.roll(x, 1, 0)

    def right(x):
        return jnp.where(lane < COLS - 1, pltpu.roll(x, COLS - 1, 1), 0.0)

    def left(x):
        return jnp.where(lane > 0, pltpu.roll(x, 1, 1), 0.0)

    trans = wide[0]
    face_row = harmonic(trans, after(trans))
    t_row[...] = face_row
    face_col = harmonic(trans, right(trans))
    t_col[...] = face_col
    diagonal = edge_f[0] + face_row + before(face_row) + face_col + left(face_col)
    inverse[...] = 1.0 / diagonal
    buoy = wide[1]
    drive = gas[...]
    push = harmonic(buoy, after(buoy)) * (after(drive) - drive)
    total = push - before(push)
    push = harmonic(buoy, right(buoy)) * (right(drive) - drive)
    total = total + (push - left(push))
    right_hand[...] = edge_f[0] * edge_f[2] + edge_f[1] + total

    for sweep in range(SWEEPS):
        pressure = edge_f[2]
        face_row = t_row[...]
        face_col = t_col[...]
        inflow = face_row * after(pressure) + before(face_row * pressure)
        inflow = inflow + (face_col * right(pressure) + left(face_col * pressure))
        edge_f[2] = (right_hand[...] + inflow) * inverse[...]

    pf[here.rows((0, 0, 0), 0, SLAB), :] = edge_f[2, pl.ds(HALO, SLAB), :]

    @pl.when(is_last)
    def _():
        pf[pl.ds(ROWS, 8), :] = edge_f[2, pl.ds(HALO + SLAB, 8), :]

    def ag_copy(q, number, flip, dim):
        rows = part_rows(q, flip)
        return pltpu.make_async_remote_copy(
            pf.at[rows], pf.at[rows], ag_send.at[q, number], ag_recv.at[q, number],
            device_id=peer(flip_of(dim)), device_id_type=MESH,
        )

    def ag_arrival(q, number, flip, dim):
        merged = tuple((a + b) % 2 for a, b in zip(flip, flip_of(dim)))
        ag_copy(q, number, merged, dim).wait_recv()

    def ag_send_one(q, number, flip, dim):
        copy = ag_copy(q, number, flip, dim)
        copy.start()
        waits.append(copy)

    for which in (2, 1, 0):
        for q in range(3):
            ag_send_one(q, (0, 0, 0)[which] if which == 2 else (3, 1, 0)[which], (0, 0, 0), ORDERS[q][which])

    def last_copy(m, other):
        return pltpu.make_async_remote_copy(
            pf.at[pl.ds(ROWS, 8)], pf.at[pl.ds(ROWS, 8)], last_send.at[m], last_recv.at[0],
            device_id=peer(other), device_id_type=MESH,
        )

    @pl.when(is_last)
    def _():
        for m, other in enumerate(OTHERS):
            last_copy(m, other).start()

    for q in range(3):
        d1, d2, d3 = ORDERS[q]
        ag_arrival(q, 0, (0, 0, 0), d3)
        ag_send_one(q, 2, flip_of(d3), d2)
        ag_send_one(q, 4, flip_of(d3), d1)
    for q in range(3):
        d1, d2, d3 = ORDERS[q]
        ag_arrival(q, 1, (0, 0, 0), d2)
        ag_send_one(q, 5, flip_of(d2), d1)
    for q in range(3):
        d1, d2, d3 = ORDERS[q]
        ag_arrival(q, 2, flip_of(d3), d2)
        ag_send_one(q, 6, flip_of(d2, d3), d1)
    for number, dims in ((3, ()), (4, (2,)), (5, (1,)), (6, (1, 2))):
        for q in range(3):
            order = ORDERS[q]
            ag_arrival(q, number, flip_of(*[order[d] for d in dims]), order[0])

    @pl.when(here.slab < 7)
    def _():
        last_copy(0, OTHERS[0]).wait_recv()

    for copy in waits:
        copy.wait_send()

    @pl.when(is_last)
    def _():
        for m, other in enumerate(OTHERS):
            last_copy(m, other).wait_send()

    @pl.when(has_up)
    def _():
        halo_up.wait_send()

    @pl.when(has_down)
    def _():
        halo_down.wait_send()

    @pl.when(area > 0)
    def _():
        row_copy(0, cond).wait_send()
        row_copy(1, hh).wait_send()

    @pl.when(crosses_up)
    def _():
        for copy in to_up:
            copy.wait_send()

    @pl.when(crosses_down)
    def _():
        for copy in to_down:
            copy.wait_send()


CHUNK = 32


def write_kernel(hh, hr, gr, hc, gc, pf, cell, rows_out, cols_out, cell_v, rows_v, cols_v, sems):
    chunks = ROWS // CHUNK

    def copies(i):
        rows = pl.ds(pl.multiple_of(i * CHUNK, 8), CHUNK)
        return [
            pltpu.make_async_copy(v.at[:, rows], o.at[:, rows], sems.at[n, i])
            for n, (v, o) in enumerate(((cell_v, cell), (rows_v, rows_out), (cols_v, cols_out)))
        ]

    @pl.loop(0, chunks)
    def _(i):
        start = pl.multiple_of(i * CHUNK, 8)
        rows = pl.ds(start, CHUNK)
        wide = pf[pl.ds(start, CHUNK + 8), :]
        pressure = wide[:CHUNK]
        row_drop = pressure - pltpu.roll(wide, CHUNK + 7, 0)[:CHUNK]
        col_drop = pressure - pltpu.roll(pressure, COLS - 1, 1)
        for k in range(LAYERS):
            cell_v[k, rows, :] = pressure + hh[k, rows, :]
            rows_v[k, rows, :] = hr[k, rows, :] * row_drop + gr[k, rows, :]
            cols_v[k, rows, :] = hc[k, rows, :] * col_drop + gc[k, rows, :]
        for copy in copies(i):
            copy.start()

    @pl.loop(0, chunks)
    def _(i):
        for copy in copies(i):
            copy.wait()


def local(permeability, mobility, thickness, caprock, plume, storage, source, pressure_old):
    f32, i32 = jnp.float32, jnp.int32
    vmem = pl.BlockSpec(memory_space=pltpu.VMEM)
    hbm = pl.BlockSpec(memory_space=pltpu.HBM)
    dma = pltpu.SemaphoreType.DMA
    V = pltpu.VMEM
    full = V((LAYERS, ROWS, COLS), f32)
    tall = V((LAYERS, ROWS + 8, COLS), f32)
    arrays = (permeability, mobility, thickness, caprock, plume, storage, source, pressure_old)
    arrays = [pltpu.with_memory_space_constraint(x, pltpu.HBM) for x in arrays]
    kept = pl.pallas_call(
        gather_kernel,
        out_shape=[tall, full, full, full, full, V((ROWS + 8, COLS), f32)],
        in_specs=[hbm] * 8,
        out_specs=[vmem] * 6,
        scratch_shapes=[
            V((LAYERS, ROWS, COLS), f32), V((LAYERS, ROWS, COLS), f32), V((LAYERS, ROWS + 8, COLS), f32),
            V((ROWS, COLS), i32), V((ROWS, COLS), i32), V((2, ROWS, COLS), f32),
            *[V((4, 2, r, COLS), f32) for r in PART_ROWS],
            *[V((2, 2, r, COLS), f32) for r in PART_ROWS],
            *[V((2, r, COLS), f32) for r in PART_ROWS],
            V((2, WIDE, COLS), f32), V((2, WIDE, COLS), i32), V((3, WIDE, COLS), f32),
            pltpu.SMEM((LAYERS,), f32), V((8, 8, 128), f32), V((32, 8, 128), f32),
            *[V((WIDE, COLS), f32) for _ in range(5)],
            dma((8, 4)), dma((3, 5)), dma((1,)), dma((3, 7)), dma((3, 7)), dma((3, 7)), dma((3, 7)),
            dma((7,)), dma((7,)), dma((2,)), dma((2,)), dma((2, 5)), dma((2, 5)), dma((2,)), dma((2,)),
            dma((7,)), dma((1,)),
        ],
        compiler_params=pltpu.CompilerParams(
            collective_id=0, has_side_effects=True, vmem_limit_bytes=26 << 20
        ),
        name="gather",
    )(*arrays)
    return pl.pallas_call(
        write_kernel,
        out_shape=[jax.ShapeDtypeStruct((LAYERS, ROWS, COLS), f32)] * 3,
        in_specs=[vmem] * 6,
        out_specs=[hbm] * 3,
        scratch_shapes=[V((LAYERS, ROWS, COLS), f32)] * 3 + [dma((3, ROWS // CHUNK))],
        compiler_params=pltpu.CompilerParams(vmem_limit_bytes=16 << 20),
        name="write",
    )(*kept)


def solution(mesh):
    in_specs = (
        P("layer", "area", None),
        P("layer", "area", None),
        P("layer"),
        P("area", None),
        P("area", None),
        P("area", None),
        P("area", None),
        P("area", None),
    )
    out_specs = (P("layer", "area", None), P("layer", "area", None), P("layer", "area", None))
    return jax.shard_map(
        lambda *args: tuple(local(*args)), mesh=mesh, in_specs=in_specs, out_specs=out_specs, check_vma=False
    )
```

time: 150 us -> 53.5 us (0.36); the launches traced: 147 us -> 53.4 us
  Pallas kernels: 0 us -> 52.7 us
  starting transfers between devices: 50.1 us -> 0 us
  other arithmetic: 46.8 us -> 0 us
  waiting for transfers between devices: 27.9 us -> 0 us
  local copies, waits for them, and re-layouts: 21.5 us -> 0 us
    pallas_call x0 -> x2, Pallas kernels: none -> 52.7 us  [the longest x1 47.7 us: local(): pl.pallas_call(gather_kernel, out_shape=[tall, full, full, full, full, V(...]
    all_to_all x3 -> x0, starting transfers between devices: 25.9 us -> none  [the longest x2 16.8 us: from_everyone(): return lax.all_to_all(copies, axis, split_axis=0, concat_axis=0, tiled=True)]
    ppermute x9 -> x0, starting transfers between devices: 24.2 us -> none  [the longest x4 17.5 us: padded_2(): lax.ppermute(last, axis, up)]
    reduce_sum x11 -> x0, other arithmetic: 20.9 us -> none  [the longest x8 10.7 us: add_block(): jnp.sum(jnp.where(gas & (depth < limit), thick_block, 0.0), axis=0)]
    all_to_all x3 -> x0, waiting for transfers between devices: 16.3 us -> none  [the longest x2 15.1 us: from_everyone(): return lax.all_to_all(copies, axis, split_axis=0, concat_axis=0, tiled=True)]
    ppermute x9 -> x0, waiting for transfers between devices: 11.6 us -> none  [the longest x4 11.6 us: padded_2(): lax.ppermute(leading, axis, [(b, a) for a, b in up])]
    while x32 -> x0, local copies, waits for them, and re-layouts: 7.75 us -> none
    mul x2 -> x0, other arithmetic: 6.84 us -> none  [the longest x1 6.8 us: local(): harmonic(conduct, side_conduct) * (cell_pressure - side_pressure)]
  transfers between devices with their start and end apart: 12 -> 0, of which waited for: 5 -> 0; matrix products, arithmetic and copies ran while one was open for 29% -> 0% of each run, Pallas kernels for 0% -> 0%
where the time goes in v1:
time: 53.5 us; the launch traced here: 53.4 us
  Pallas kernels  52.7 us (99%)
  between operations  0.64 us (1%)
    pallas_call x1, Pallas kernels, local(): pl.pallas_call(gather_kernel, out_shape=[tall, full, full, full, full, V(...  47.7 us
    pallas_call x1, Pallas kernels, local(): pl.pallas_call(write_kernel, out_shape=[jax.ShapeDtypeStruct((LAYERS, ROW...  5.02 us

profile of v1, /device:TPU:0, one launch (start us, length us, event | category | flops | bytes accessed | tf_op | source)
XLA Modules:
  0.0 53.4 jit_solution(15435033253051325622)
XLA Ops:
  0.6 47.7 %gather.1 = (f32[4,520,512]{2,1,0:T(8,128)S(1)}, f32[4,512,512]{2,1,0:T(8,128)S(1)}, f32[4,512,512]{2,1,0:T(8,128)S(1)}, f32[4,512,512]{2,1,0:T(8,128)S(1)}, f32...) custom-call(f32[4,512,512]{2,1,0:T(8,128)} %perm.1, f32[4,512,512]{2,1,0:T(8,128)} %mob.1, f32[4]{0:T(128)} %thick.1, ...), custom_call_target="tpu_custom_call" | custom-call | tf_op jit(solution)/shard_map/gather/pallas_call | solution.py:626
  48.4 5.0 %write.1 = (f32[4,512,512]{2,1,0:T(8,128)}, f32[4,512,512]{2,1,0:T(8,128)}, f32[4,512,512]{2,1,0:T(8,128)}) custom-call(f32[4,520,512]{2,1,0:T(8,128)S(1)} %get-tuple-element.9.hh, f32[4,512,512]{2,1,0:T(8,128)S(1)} %get-tuple-element.10.hr, f32[4,512,512]{2,1,0:T(8,128)S(1)} %get-tuple-element.11.gr, f32[4,512,512]{2,1,0:T(8,128)S(1)} %get-tuple-element.12.hc, ...), custom_call_target="tpu_custom_call" | custom-call | tf_op jit(solution)/shard_map/write/pallas_call | solution.py:649

commit v2 on v1

--- a/solution.py
+++ b/solution.py
@@ -76,8 +76,10 @@
     perm, mob, thick, cap, plu, sto, src, old,
     hh, hr, gr, hc, gc, pf,
     permv, mobv, cond, capv, pluv, tb, r1a, r1b, r1c, r2a, r2b, r2c, r3a, r3b, r3c,
+    edge_3d, edge_2d, tiles, parts, sums, cross,
     wide, edge_i, edge_f, thick_s, thick_all, table, gas, t_row, t_col, right_hand, inverse,
     in_sem, edge_sem, thick_sem, rs_send, rs_recv, ag_send, ag_recv, th_send, th_recv,
+    part_load, part_send, part_recv, sum_send, sum_recv, ready,
     halo_send, halo_recv, input_send, input_recv, row_send, row_recv, last_send, last_recv,
 ):
     here = Place()
@@ -93,6 +95,17 @@
     loads = []
     thick_copy = pltpu.make_async_copy(thick, thick_s, thick_sem.at[0])
     thick_copy.start()
+    part_copies = []
+    for side, first_row in ((0, 0), (1, ROWS - HALO)):
+        rows = pl.ds(first_row, HALO)
+        part_copies += [
+            pltpu.make_async_copy(cap.at[rows], edge_2d.at[0, side], part_load.at[side, 0]),
+            pltpu.make_async_copy(plu.at[rows], edge_2d.at[1, side], part_load.at[side, 1]),
+            pltpu.make_async_copy(perm.at[:, rows], edge_3d.at[0, side], part_load.at[side, 2]),
+            pltpu.make_async_copy(mob.at[:, rows], edge_3d.at[1, side], part_load.at[side, 3]),
+        ]
+    for copy in part_copies:
+        copy.start()
     for n, flip in enumerate(FLIPS):
         rows = here.rows(flip, 0, SLAB)
         group = [
@@ -108,10 +121,12 @@
     barrier = pltpu.get_barrier_semaphore()
     for flip in OTHERS:
         pl.semaphore_signal(barrier, inc=1, device_id=peer(flip), device_id_type=MESH)
-    for step in (1, here.areas - 1):
-        pl.semaphore_signal(
-            barrier, inc=1, device_id=((area + step) % here.areas, layer), device_id_type=MESH
-        )
+    both_sides = [((area + step) % here.areas, layer) for step in (1, here.areas - 1)]
+
+    @pl.when(here.parity == 0)
+    def _():
+        for neighbour in both_sides:
+            pl.semaphore_signal(barrier, inc=1, device_id=neighbour, device_id_type=MESH)
 
     base = here.slab * SLAB
     sources = (cap, plu, sto, src, old)
@@ -170,6 +185,50 @@
     top_edge = is_first & (area == 0)
     bottom_edge = is_last & (area == here.areas - 1)
 
+    sub8 = lax.broadcasted_iota(jnp.int32, (8, COLS), 0)
+    for copy in part_copies:
+        copy.wait()
+    for side in (0, 1):
+        top = edge_2d[0, side]
+        bottom = edge_2d[1, side]
+        trans = buoy = jnp.zeros((8, COLS), jnp.float32)
+        for k in range(LAYERS):
+            depth = layer * LAYERS + k
+            flow = edge_3d[0, side, k] * edge_3d[1, side, k] * thick_s[k]
+            flow = jnp.where(depth >= top, flow, 0.0)
+            trans = trans + flow
+            buoy = buoy + jnp.where(depth < bottom, flow, 0.0)
+        used = (sub8 < 4) if side == 0 else (sub8 >= 4)
+        tiles[side] = jnp.where(used, trans, pltpu.roll(buoy, 4, 0))
+
+    pl.semaphore_wait(barrier, 7 + 2 * here.parity)
+
+    @pl.when(here.parity == 1)
+    def _():
+        for neighbour in both_sides:
+            pl.semaphore_signal(ready, inc=1, device_id=neighbour, device_id_type=MESH)
+
+    def part_copy(m, side):
+        return pltpu.make_async_remote_copy(
+            tiles.at[side], parts.at[m], part_send.at[side], part_recv.at[m],
+            device_id=peer(OTHERS[m]), device_id_type=MESH,
+        )
+
+    for m, other in enumerate(OTHERS):
+        for side, owner in ((0, 0), (1, 7)):
+
+            @pl.when(here.slab_of(other) == owner)
+            def _(m=m, side=side):
+                part_copy(m, side).start()
+
+    for m, other in enumerate(OTHERS):
+        copy = pltpu.make_async_remote_copy(
+            thick_all.at[layer], thick_all.at[layer], th_send.at[m], th_recv.at[m],
+            device_id=peer(other), device_id_type=MESH,
+        )
+        copy.start()
+        waits.append(copy)
+
     def conduct_slab(n, flip):
         for copy in loads[n]:
             copy.wait()
@@ -220,32 +279,12 @@
 
     for n, flip in enumerate(FLIPS):
         conduct_slab(n, flip)
-        if n == 0:
-            pl.semaphore_wait(barrier, 9)
         for q in range(3):
             for m in range(4):
                 owner, copy = first_copy(q, m)
                 if owner == flip:
                     copy.start()
                     waits.append(copy)
-        if n == 0:
-            for m, other in enumerate(OTHERS):
-                copy = pltpu.make_async_remote_copy(
-                    thick_all.at[layer], thick_all.at[layer], th_send.at[m], th_recv.at[m],
-                    device_id=peer(other), device_id_type=MESH,
-                )
-                copy.start()
-                waits.append(copy)
-
-            @pl.when(crosses_up)
-            def _():
-                for copy in to_up:
-                    copy.start()
-
-            @pl.when(crosses_down)
-            def _():
-                for copy in to_down:
-                    copy.start()
 
     def row_copy(n, array):
         return pltpu.make_async_remote_copy(
@@ -253,37 +292,20 @@
             device_id=(area - 1, layer), device_id_type=MESH,
         )
 
-    @pl.when(area > 0)
-    def _():
-        row_copy(0, cond).start()
-
-    for m, other in enumerate(OTHERS):
-        pltpu.make_async_remote_copy(
-            thick_all.at[layer], thick_all.at[here.layer_of(other)], th_send.at[m], th_recv.at[m],
-            device_id=peer(other), device_id_type=MESH,
-        ).wait_recv()
-    for block in range(8):
-        for k in range(LAYERS):
-            table[block * LAYERS + k] = jnp.broadcast_to(
-                thick_all[block, pl.ds(k, 1), :], (8, 128)
-            )
-
     def across(tile):
         return jnp.concatenate([tile] * (COLS // 128), axis=1)
 
-    over_all = lax.fori_loop(
-        0, layer * LAYERS, lambda z, total: total + table[z], jnp.zeros((8, 128), jnp.float32)
-    )
-
     def gas_sum(blocks, top, bottom):
-        def add_block(block, total):
-            for k in range(LAYERS):
-                depth = block * LAYERS + k
-                inside = (depth >= top) & (depth < bottom)
-                total = total + jnp.where(inside, across(table[depth]), 0.0)
-            return total
-
-        return lax.fori_loop(0, blocks, add_block, jnp.zeros(top.shape, jnp.float32))
+        def lookup(index, count):
+            def step(block, found):
+                for k in range(LAYERS):
+                    depth = block * LAYERS + k
+                    found = jnp.where(depth < index, across(table[depth + 1]), found)
+                return found
+
+            return lax.fori_loop(0, count, step, jnp.zeros(index.shape, jnp.float32))
+
+        return jnp.maximum(lookup(bottom, blocks) - lookup(top, jnp.minimum(blocks, 4)), 0.0)
 
     def heads(low, high):
         @pl.loop(low, high)
@@ -291,7 +313,7 @@
             rows = pl.ds(pl.multiple_of(i * 8, 8), 8)
             top = capv[rows, :]
             bottom = pluv[rows, :]
-            above = across(over_all) - (brine_density - gas_density) * gas_sum(layer, top, bottom)
+            above = across(table[layer * LAYERS]) - (brine_density - gas_density) * gas_sum(layer, top, bottom)
             for k in range(LAYERS):
                 depth = layer * LAYERS + k
                 inside = (depth >= top) & (depth < bottom)
@@ -332,14 +354,71 @@
             copy.start()
             waits.append(copy)
 
+    forward_up = pltpu.make_async_remote_copy(
+        sums, cross.at[1], sum_send.at[0], sum_recv.at[1],
+        device_id=(area - 1, layer), device_id_type=MESH,
+    )
+    forward_down = pltpu.make_async_remote_copy(
+        sums, cross.at[0], sum_send.at[0], sum_recv.at[0],
+        device_id=(area + 1, layer), device_id_type=MESH,
+    )
+
+    def forward_edges():
+        for ends, side in ((is_first, 0), (is_last, 1)):
+
+            @pl.when(ends)
+            def _(side=side):
+                for m in range(7):
+                    part_copy(m, side).wait_recv()
+                total = tiles[side]
+                for m in range(7):
+                    total = total + parts[m]
+                sums[...] = total
+
+        @pl.when(crosses_up)
+        def _():
+            for copy in (forward_up, *to_up):
+                copy.start()
+
+        @pl.when(crosses_down)
+        def _():
+            for copy in (forward_down, *to_down):
+                copy.start()
+
+        @pl.when(area > 0)
+        def _():
+            row_copy(0, cond).start()
+
+    def gas_rows(at):
+        rows = pl.ds(at, 8)
+        gas[rows, :] = buoyancy_scale * gas_sum(8, edge_i[0, rows, :], edge_i[1, rows, :])
+
+    @pl.when(here.parity == 1)
+    def _():
+        forward_edges()
+
     second(0)
+
+    for m, other in enumerate(OTHERS):
+        pltpu.make_async_remote_copy(
+            thick_all.at[layer], thick_all.at[here.layer_of(other)], th_send.at[m], th_recv.at[m],
+            device_id=peer(other), device_id_type=MESH,
+        ).wait_recv()
+    total = jnp.zeros((8, 128), jnp.float32)
+    table[0] = total
+    for block in range(8):
+        for k in range(LAYERS):
+            total = total + jnp.broadcast_to(thick_all[block, pl.ds(k, 1), :], (8, 128))
+            table[block * LAYERS + k + 1] = total
+
+
+    second(1)
     heads(0, 32)
-    second(1)
-    heads(32, 64)
-
-    @pl.when(area > 0)
-    def _():
-        row_copy(1, hh).start()
+
+    @pl.when(here.parity == 0)
+    def _():
+        pl.semaphore_wait(ready, 2)
+        forward_edges()
 
     for copy in mid_copies:
         copy.wait()
@@ -353,39 +432,6 @@
     def _():
         for copy in edge_copies(2, SLAB, HALO, HALO + SLAB):
             copy.wait()
-
-    @pl.when(crosses_up)
-    def _():
-        for copy in to_down:
-            copy.wait_recv()
-
-    @pl.when(crosses_down)
-    def _():
-        for copy in to_up:
-            copy.wait_recv()
-
-    def blank(at):
-        rows = pl.ds(at, HALO)
-        edge_i[:, rows, :] = jnp.zeros((2, HALO, COLS), jnp.int32)
-        edge_f[0, rows, :] = jnp.ones((HALO, COLS), jnp.float32)
-        edge_f[1, rows, :] = jnp.zeros((HALO, COLS), jnp.float32)
-        edge_f[2, rows, :] = jnp.zeros((HALO, COLS), jnp.float32)
-        wide[:, rows, :] = jnp.zeros((2, HALO, COLS), jnp.float32)
-
-    @pl.when(top_edge)
-    def _():
-        blank(0)
-
-    @pl.when(bottom_edge)
-    def _():
-        blank(HALO + SLAB)
-
-    @pl.loop(0, WIDE // 8)
-    def _(i):
-        rows = pl.ds(pl.multiple_of(i * 8, 8), 8)
-        gas[rows, :] = buoyancy_scale * gas_sum(8, edge_i[0, rows, :], edge_i[1, rows, :])
-
-    faces(0, 5)
 
     for q in range(3):
         first_copy(q, 2)[1].wait_recv()
@@ -396,19 +442,15 @@
         copy.start()
         waits.append(copy)
 
-    faces(5, 15)
-
-    @pl.when(area < here.areas - 1)
-    def _():
-        row_copy(0, cond).wait_recv()
-        row_copy(1, hh).wait_recv()
-
-    @pl.when(area == here.areas - 1)
-    def _():
-        cond[:, pl.ds(ROWS, 8), :] = jnp.zeros((LAYERS, 8, COLS), jnp.float32)
-        hh[:, pl.ds(ROWS, 8), :] = jnp.zeros((LAYERS, 8, COLS), jnp.float32)
-
-    faces(15, 16)
+    heads(32, 64)
+
+    @pl.when(area > 0)
+    def _():
+        row_copy(1, hh).start()
+
+    @pl.loop(1, WIDE // 8 - 1)
+    def _(i):
+        gas_rows(pl.multiple_of(i * 8, 8))
 
     for q in range(3):
         first_copy(q, 3)[1].wait_recv()
@@ -418,36 +460,67 @@
         at = pl.ds(HALO + PART_START[q], PART_ROWS[q])
         wide[:, at, :] = tb[:, mine, :] + r1[q][3] + (r2[q][1] + r3[q][...])
 
-    up_area = area - (7 - here.slab) // 7
-    up_same = 1 - (7 - here.slab) // 7
-    down_area = area + here.slab // 7
-    down_same = 1 - here.slab // 7
-    up_layer = up_same * here.layer_of_slab(here.slab - up_same) + (1 - up_same) * layer
-    down_layer = down_same * here.layer_of_slab(here.slab + down_same) + (1 - down_same) * layer
+    up_layer = here.layer_of_slab(jnp.maximum(here.slab - 1, 0))
+    down_layer = here.layer_of_slab(jnp.minimum(here.slab + 1, 7))
     halo_up = pltpu.make_async_remote_copy(
         wide.at[:, pl.ds(HALO, HALO)], wide.at[:, pl.ds(HALO + SLAB, HALO)],
-        halo_send.at[0], halo_recv.at[0], device_id=(up_area, up_layer), device_id_type=MESH,
+        halo_send.at[0], halo_recv.at[0], device_id=(area, up_layer), device_id_type=MESH,
     )
     halo_down = pltpu.make_async_remote_copy(
         wide.at[:, pl.ds(SLAB, HALO)], wide.at[:, pl.ds(0, HALO)],
-        halo_send.at[1], halo_recv.at[1], device_id=(down_area, down_layer), device_id_type=MESH,
+        halo_send.at[1], halo_recv.at[1], device_id=(area, down_layer), device_id_type=MESH,
     )
-    has_up = area * 8 + here.slab > 0
-    has_down = area * 8 + here.slab < here.areas * 8 - 1
-
-    @pl.when(has_up)
+
+    @pl.when(here.slab > 0)
     def _():
         halo_up.start()
 
-    @pl.when(has_down)
+    @pl.when(here.slab < 7)
     def _():
         halo_down.start()
 
-    @pl.when(has_up)
+    def blank(at):
+        rows = pl.ds(at, HALO)
+        edge_i[:, rows, :] = jnp.zeros((2, HALO, COLS), jnp.int32)
+        edge_f[0, rows, :] = jnp.ones((HALO, COLS), jnp.float32)
+        edge_f[1, rows, :] = jnp.zeros((HALO, COLS), jnp.float32)
+        edge_f[2, rows, :] = jnp.zeros((HALO, COLS), jnp.float32)
+        wide[:, rows, :] = jnp.zeros((2, HALO, COLS), jnp.float32)
+
+    def unpack(slot, at, used):
+        rows = pl.ds(at, HALO)
+        tile = cross[slot]
+        wide[0, rows, :] = jnp.where(used, tile, 0.0)
+        wide[1, rows, :] = jnp.where(used, pltpu.roll(tile, 4, 0), 0.0)
+
+    @pl.when(top_edge)
+    def _():
+        blank(0)
+
+    @pl.when(bottom_edge)
+    def _():
+        blank(HALO + SLAB)
+
+    @pl.when(crosses_up)
+    def _():
+        for copy in (forward_down, *to_down):
+            copy.wait_recv()
+        unpack(0, 0, sub8 >= 4)
+
+    @pl.when(crosses_down)
+    def _():
+        for copy in (forward_up, *to_up):
+            copy.wait_recv()
+        unpack(1, HALO + SLAB, sub8 < 4)
+
+    gas_rows(0)
+    gas_rows(HALO + SLAB)
+
+    @pl.when(here.slab > 0)
     def _():
         halo_down.wait_recv()
 
-    @pl.when(has_down)
+    @pl.when(here.slab < 7)
     def _():
         halo_up.wait_recv()
 
@@ -525,19 +598,35 @@
         for m, other in enumerate(OTHERS):
             last_copy(m, other).start()
 
+    faces(0, 4)
     for q in range(3):
         d1, d2, d3 = ORDERS[q]
         ag_arrival(q, 0, (0, 0, 0), d3)
         ag_send_one(q, 2, flip_of(d3), d2)
         ag_send_one(q, 4, flip_of(d3), d1)
+    faces(4, 8)
     for q in range(3):
         d1, d2, d3 = ORDERS[q]
         ag_arrival(q, 1, (0, 0, 0), d2)
         ag_send_one(q, 5, flip_of(d2), d1)
+    faces(8, 11)
     for q in range(3):
         d1, d2, d3 = ORDERS[q]
         ag_arrival(q, 2, flip_of(d3), d2)
         ag_send_one(q, 6, flip_of(d2, d3), d1)
+    faces(11, 15)
+
+    @pl.when(area < here.areas - 1)
+    def _():
+        row_copy(0, cond).wait_recv()
+        row_copy(1, hh).wait_recv()
+
+    @pl.when(area == here.areas - 1)
+    def _():
+        cond[:, pl.ds(ROWS, 8), :] = jnp.zeros((LAYERS, 8, COLS), jnp.float32)
+        hh[:, pl.ds(ROWS, 8), :] = jnp.zeros((LAYERS, 8, COLS), jnp.float32)
+
+    faces(15, 16)
     for number, dims in ((3, ()), (4, (2,)), (5, (1,)), (6, (1, 2))):
         for q in range(3):
             order = ORDERS[q]
@@ -555,13 +644,21 @@
         for m, other in enumerate(OTHERS):
             last_copy(m, other).wait_send()
 
-    @pl.when(has_up)
+    @pl.when(here.slab > 0)
     def _():
         halo_up.wait_send()
 
-    @pl.when(has_down)
+    @pl.when(here.slab < 7)
     def _():
         halo_down.wait_send()
+
+    @pl.when(is_first == False)
+    def _():
+        part_copy(0, 0).wait_send()
+
+    @pl.when(is_last == False)
+    def _():
+        part_copy(0, 1).wait_send()
 
     @pl.when(area > 0)
     def _():
@@ -570,12 +667,12 @@
 
     @pl.when(crosses_up)
     def _():
-        for copy in to_up:
+        for copy in (forward_up, *to_up):
             copy.wait_send()
 
     @pl.when(crosses_down)
     def _():
-        for copy in to_down:
+        for copy in (forward_down, *to_down):
             copy.wait_send()
 
 
@@ -634,11 +731,15 @@
             *[V((4, 2, r, COLS), f32) for r in PART_ROWS],
             *[V((2, 2, r, COLS), f32) for r in PART_ROWS],
             *[V((2, r, COLS), f32) for r in PART_ROWS],
+            V((2, 2, LAYERS, 8, COLS), f32), V((2, 2, 8, COLS), i32), V((2, 8, COLS), f32),
+            V((7, 8, COLS), f32), V((8, COLS), f32), V((2, 8, COLS), f32),
             V((2, WIDE, COLS), f32), V((2, WIDE, COLS), i32), V((3, WIDE, COLS), f32),
-            pltpu.SMEM((LAYERS,), f32), V((8, 8, 128), f32), V((32, 8, 128), f32),
+            pltpu.SMEM((LAYERS,), f32), V((8, 8, 128), f32), V((33, 8, 128), f32),
             *[V((WIDE, COLS), f32) for _ in range(5)],
             dma((8, 4)), dma((3, 5)), dma((1,)), dma((3, 7)), dma((3, 7)), dma((3, 7)), dma((3, 7)),
-            dma((7,)), dma((7,)), dma((2,)), dma((2,)), dma((2, 5)), dma((2, 5)), dma((2,)), dma((2,)),
+            dma((7,)), dma((7,)),
+            dma((2, 4)), dma((2,)), dma((7,)), dma((1,)), dma((2,)), pltpu.SemaphoreType.REGULAR,
+            dma((2,)), dma((2,)), dma((2, 5)), dma((2, 5)), dma((2,)), dma((2,)),
             dma((7,)), dma((1,)),
         ],
         compiler_params=pltpu.CompilerParams(

time: 53.5 us -> 50.9 us (0.951)
  Pallas kernels: 52.7 us -> 50.1 us
    pallas_call x1, Pallas kernels: 47.7 us -> 45.1 us  [local(): pl.pallas_call(gather_kernel, out_shape=[tall, full, full, full, full, V(...]
where the time goes in v2:
time: 50.9 us; the launch traced here: 50.8 us
  Pallas kernels  50.1 us (98%)
  between operations  0.64 us (1%)
    pallas_call x1, Pallas kernels, local(): pl.pallas_call(gather_kernel, out_shape=[tall, full, full, full, full, V(...  45.1 us
    pallas_call x1, Pallas kernels, local(): pl.pallas_call(write_kernel, out_shape=[jax.ShapeDtypeStruct((LAYERS, ROW...  5.02 us

profile of v2, /device:TPU:0, one launch (start us, length us, event | category | flops | bytes accessed | tf_op | source)
XLA Modules:
  0.0 50.8 jit_solution(13756482630801593850)
XLA Ops:
  0.6 45.1 %gather.1 = (f32[4,520,512]{2,1,0:T(8,128)S(1)}, f32[4,512,512]{2,1,0:T(8,128)S(1)}, f32[4,512,512]{2,1,0:T(8,128)S(1)}, f32[4,512,512]{2,1,0:T(8,128)S(1)}, f32...) custom-call(f32[4,512,512]{2,1,0:T(8,128)} %perm.1, f32[4,512,512]{2,1,0:T(8,128)} %mob.1, f32[4]{0:T(128)} %thick.1, ...), custom_call_target="tpu_custom_call" | custom-call | tf_op jit(solution)/shard_map/gather/pallas_call | solution.py:723
  45.8 5.0 %write.1 = (f32[4,512,512]{2,1,0:T(8,128)}, f32[4,512,512]{2,1,0:T(8,128)}, f32[4,512,512]{2,1,0:T(8,128)}) custom-call(f32[4,520,512]{2,1,0:T(8,128)S(1)} %get-tuple-element.9.hh, f32[4,512,512]{2,1,0:T(8,128)S(1)} %get-tuple-element.10.hr, f32[4,512,512]{2,1,0:T(8,128)S(1)} %get-tuple-element.11.gr, f32[4,512,512]{2,1,0:T(8,128)S(1)} %get-tuple-element.12.hc, ...), custom_call_target="tpu_custom_call" | custom-call | tf_op jit(solution)/shard_map/write/pallas_call | solution.py:750

commit v3 on v2

v3 whole, which is shorter than its diff:
```python
import functools

import jax
import jax.numpy as jnp
from jax import lax
from jax.experimental import pallas as pl
from jax.experimental.pallas import tpu as pltpu
from jax.sharding import PartitionSpec as P

SWEEPS = 3
buoyancy_scale = 0.3
gravity_scale = 0.05
gas_density = 0.7
brine_density = 1.0

LAYERS = 4
ROWS = 512
COLS = 512
HALVES = 2
HALF_ROWS = ROWS // HALVES
SLAB = 32
HALO = 8
WIDE = SLAB + 2 * HALO
MESH = pl.DeviceIdType.MESH

ORDERS = ((0, 1, 2), (1, 2, 0), (2, 0, 1))
PART_START = ((0, 16, 24), (0, 8, 24))
PART_ROWS = ((16, 8, 8), (8, 16, 8))
X_FIRST = (16, 8)
ACROSS = ((1, 1, 0), (1, 0, 0), (0, 1, 0))
OTHER_HALF = (0, 0, 1)
OWN = (0, 0, 0)
FLIPS = ((1, 1, 1), (1, 1, 0), (0, 1, 1), (1, 0, 1), (1, 0, 0), (0, 1, 0), (0, 0, 1), (0, 0, 0))
OTHERS = FLIPS[:-1]


def harmonic(near_value, far_value):
    summed = near_value + far_value
    divisor = jnp.where(summed > 0, summed, 1.0)
    return 2.0 * near_value * far_value / divisor


def flip_of(*dims):
    return tuple(1 if d in dims else 0 for d in range(3))


def plus(one, two):
    return tuple((a + b) % 2 for a, b in zip(one, two))


class Place:
    def __init__(self):
        self.area = lax.axis_index("area")
        self.layer = lax.axis_index("layer")
        self.areas = lax.axis_size("area")
        x = self.layer % 4
        second = x // 2
        first = (x % 2) + second - 2 * (x % 2) * second
        self.code = (first, second, self.layer // 4)
        self.parity = self.area % 2
        self.order = self.order_of(OWN)

    def flipped(self, flip):
        return tuple((1 - c) if f else c for c, f in zip(self.code, flip))

    def layer_of(self, flip):
        first, second, half = self.flipped(flip)
        x = 2 * second + first + second - 2 * first * second
        return half * 4 + x

    def order_of(self, flip):
        first, second, half = self.flipped(flip)
        x = 2 * second + first + second - 2 * first * second
        return x + half * (7 - 2 * x)

    def layer_at(self, order):
        return order + (order // 4) * (11 - 2 * order)

    def base(self, h, flip):
        order = self.order_of(flip)
        return h * HALF_ROWS + (7 - order if h else order) * SLAB

    def rows(self, h, flip, start, count):
        return pl.ds(pl.multiple_of(self.base(h, flip) + start, 8), count)


def gather_kernel(*refs):
    perm, mob, thick, cap, plu, sto, src, old = refs[:8]
    hh, hr, gr, hc, gc, pf = refs[8:14]
    r1 = [refs[14 + 3 * h : 17 + 3 * h] for h in range(HALVES)]
    r2 = [refs[20 + 3 * h : 23 + 3 * h] for h in range(HALVES)]
    r3 = [refs[26 + 3 * h : 29 + 3 * h] for h in range(HALVES)]
    (
        permv, mobv, cond, capv, pluv, tb,
        edge_3d, edge_2d, tiles, parts, sums, cross,
        wide, edge_i, edge_f, thick_s, thick_all, table, gas, t_row, t_col, right_hand, inverse,
        in_sem, edge_sem, thick_sem, rs_send, rs_recv, ag_send, ag_recv, th_send, th_recv,
        part_load, part_send, part_recv, sum_send, sum_recv, ready,
        halo_send, halo_recv, input_send, input_recv, row_send, row_recv, last_send, last_recv,
    ) = refs[32:]
    here = Place()
    area, layer = here.area, here.layer
    waits = []
    at_ends = here.order == 0
    at_middle = here.order == 7

    def peer(flip):
        return (area, here.layer_of(flip))

    loads = []
    thick_copy = pltpu.make_async_copy(thick, thick_s, thick_sem.at[0])
    thick_copy.start()
    part_copies = []
    for side, first_row in enumerate((0, ROWS - HALO, HALF_ROWS, HALF_ROWS - HALO)):
        rows = pl.ds(first_row, HALO)
        part_copies += [
            pltpu.make_async_copy(cap.at[rows], edge_2d.at[0, side], part_load.at[side, 0]),
            pltpu.make_async_copy(plu.at[rows], edge_2d.at[1, side], part_load.at[side, 1]),
            pltpu.make_async_copy(perm.at[:, rows], edge_3d.at[0, side], part_load.at[side, 2]),
            pltpu.make_async_copy(mob.at[:, rows], edge_3d.at[1, side], part_load.at[side, 3]),
        ]
    for copy in part_copies:
        copy.start()
    blocks = [(h, flip) for h in range(HALVES) for flip in FLIPS]
    for n, (h, flip) in enumerate(blocks):
        rows = here.rows(h, flip, 0, SLAB)
        group = [
            pltpu.make_async_copy(cap.at[rows], capv.at[rows], in_sem.at[n, 0]),
            pltpu.make_async_copy(plu.at[rows], pluv.at[rows], in_sem.at[n, 1]),
            pltpu.make_async_copy(perm.at[:, rows], permv.at[:, rows], in_sem.at[n, 2]),
            pltpu.make_async_copy(mob.at[:, rows], mobv.at[:, rows], in_sem.at[n, 3]),
        ]
        for copy in group:
            copy.start()
        loads.append(group)

    barrier = pltpu.get_barrier_semaphore()
    for flip in OTHERS:
        pl.semaphore_signal(barrier, inc=1, device_id=peer(flip), device_id_type=MESH)
    both_sides = [((area + step) % here.areas, layer) for step in (1, here.areas - 1)]

    @pl.when(here.parity == 0)
    def _():
        for neighbour in both_sides:
            pl.semaphore_signal(barrier, inc=1, device_id=neighbour, device_id_type=MESH)

    sources = (cap, plu, sto, src, old)

    def edge_targets(h):
        return (edge_i.at[h, 0], edge_i.at[h, 1], edge_f.at[h, 0], edge_f.at[h, 1], edge_f.at[h, 2])

    def edge_copies(sem_row, h, at, count):
        rows = here.rows(h, OWN, at - HALO, count)
        return [
            pltpu.make_async_copy(s.at[rows], t.at[pl.ds(at, count)], edge_sem.at[sem_row, n])
            for n, (s, t) in enumerate(zip(sources, edge_targets(h)))
        ]

    always = [edge_copies(0, 0, HALO, SLAB + HALO), edge_copies(1, 1, 0, SLAB + HALO)]

    def sometimes(h):
        return edge_copies(2 + h, h, h * (HALO + SLAB), HALO)

    for copy in (*always[0], *always[1]):
        copy.start()

    @pl.when(here.order > 0)
    def _():
        for h in range(HALVES):
            for copy in sometimes(h):
                copy.start()

    thick_copy.wait()
    sublane = lax.broadcasted_iota(jnp.int32, (8, 128), 0)
    tile = jnp.zeros((8, 128), jnp.float32)
    for k in range(LAYERS):
        tile = jnp.where(sublane == k, thick_s[k], tile)
    thick_all[layer] = tile

    def input_sends():
        up = [
            pltpu.make_async_remote_copy(
                s.at[pl.ds(0, HALO)], t.at[pl.ds(HALO + SLAB, HALO)],
                input_send.at[0, n], input_recv.at[0, n],
                device_id=(area - 1, layer), device_id_type=MESH,
            )
            for n, (s, t) in enumerate(zip(sources, edge_targets(1)))
        ]
        down = [
            pltpu.make_async_remote_copy(
                s.at[pl.ds(ROWS - HALO, HALO)], t.at[pl.ds(0, HALO)],
                input_send.at[1, n], input_recv.at[1, n],
                device_id=(area + 1, layer), device_id_type=MESH,
            )
            for n, (s, t) in enumerate(zip(sources, edge_targets(0)))
        ]
        return up, down

    to_up, to_down = input_sends()
    crosses_up = at_ends & (area > 0)
    crosses_down = at_ends & (area < here.areas - 1)
    top_edge = at_ends & (area == 0)
    bottom_edge = at_ends & (area == here.areas - 1)

    sub8 = lax.broadcasted_iota(jnp.int32, (8, COLS), 0)
    for copy in part_copies:
        copy.wait()
    for side in range(4):
        top = edge_2d[0, side]
        bottom = edge_2d[1, side]
        trans = buoy = jnp.zeros((8, COLS), jnp.float32)
        for k in range(LAYERS):
            depth = layer * LAYERS + k
            flow = edge_3d[0, side, k] * edge_3d[1, side, k] * thick_s[k]
            flow = jnp.where(depth >= top, flow, 0.0)
            trans = trans + flow
            buoy = buoy + jnp.where(depth < bottom, flow, 0.0)
        used = (sub8 < 4) if side % 2 == 0 else (sub8 >= 4)
        tiles[side // 2, side % 2] = jnp.where(used, trans, pltpu.roll(buoy, 4, 0))

    pl.semaphore_wait(barrier, 7 + 2 * here.parity)

    @pl.when(here.parity == 1)
    def _():
        for neighbour in both_sides:
            pl.semaphore_signal(ready, inc=1, device_id=neighbour, device_id_type=MESH)

    def part_copy(m, pair):
        return pltpu.make_async_remote_copy(
            tiles.at[pair], parts.at[m], part_send.at[pair], part_recv.at[m],
            device_id=peer(OTHERS[m]), device_id_type=MESH,
        )

    for m, other in enumerate(OTHERS):
        for pair, owner in ((0, 0), (1, 7)):

            @pl.when(here.order_of(other) == owner)
            def _(m=m, pair=pair):
                part_copy(m, pair).start()

    for m, other in enumerate(OTHERS):
        copy = pltpu.make_async_remote_copy(
            thick_all.at[layer], thick_all.at[layer], th_send.at[m], th_recv.at[m],
            device_id=peer(other), device_id_type=MESH,
        )
        copy.start()
        waits.append(copy)

    def conduct_slab(n, h, flip):
        for copy in loads[n]:
            copy.wait()
        start = here.base(h, flip)

        @pl.loop(0, SLAB // 8)
        def _(i):
            rows = pl.ds(pl.multiple_of(start + i * 8, 8), 8)
            top = capv[rows, :]
            bottom = pluv[rows, :]
            trans = None
            for k in range(LAYERS):
                depth = layer * LAYERS + k
                flow = permv[k, rows, :] * mobv[k, rows, :] * thick_s[k]
                flow = jnp.where(depth >= top, flow, 0.0)
                cond[k, rows, :] = flow
                part = jnp.where(depth < bottom, flow, 0.0)
                trans, buoy = (flow, part) if trans is None else (trans + flow, buoy + part)
            tb[0, rows, :] = trans
            tb[1, rows, :] = buoy

    def rs_copy(h, q, number, rows, buffer, dim):
        return pltpu.make_async_remote_copy(
            tb.at[:, rows], buffer, rs_send.at[3 * h + q, number], rs_recv.at[3 * h + q, number],
            device_id=peer(flip_of(dim)), device_id_type=MESH,
        )

    PIECES = ((1, 1), (1, 0), (0, 1), (0, 0))

    def part_rows(h, q, flip):
        return here.rows(h, flip, PART_START[h][q], PART_ROWS[h][q])

    def first_copy(h, q, n):
        d1, d2, d3 = ORDERS[q]
        e2, e3 = PIECES[n]
        flip = flip_of(*([d1] + [d2] * e2 + [d3] * e3))
        return flip, rs_copy(h, q, n, part_rows(h, q, flip), r1[h][q].at[n], d1)

    def second_copy(h, q, n):
        d1, d2, d3 = ORDERS[q]
        flip = flip_of(*([d2] + ([d3] if n == 0 else [])))
        return rs_copy(h, q, 4 + n, part_rows(h, q, flip), r2[h][q].at[n], d2), flip

    def third_copy(h, q):
        flip = flip_of(ORDERS[q][2])
        return rs_copy(h, q, 6, part_rows(h, q, flip), r3[h][q], ORDERS[q][2]), flip

    def send(copy):
        copy.start()
        waits.append(copy)

    later = []
    for n, (h, flip) in enumerate(blocks):
        conduct_slab(n, h, flip)
        for q in range(3):
            for m in range(4):
                owner, copy = first_copy(h, q, m)
                if owner == flip:
                    if h == 0 or m < 2:
                        send(copy)
                    else:
                        later.append(copy)

    def row_copy(n, array):
        return pltpu.make_async_remote_copy(
            array.at[:, pl.ds(0, 8)], array.at[:, pl.ds(ROWS, 8)], row_send.at[n], row_recv.at[n],
            device_id=(area - 1, layer), device_id_type=MESH,
        )

    def across(tile):
        return jnp.concatenate([tile] * (COLS // 128), axis=1)

    def gas_sum(blocks, top, bottom):
        def lookup(index, count):
            def step(block, found):
                for k in range(LAYERS):
                    depth = block * LAYERS + k
                    found = jnp.where(depth < index, across(table[depth + 1]), found)
                return found

            return lax.fori_loop(0, count, step, jnp.zeros(index.shape, jnp.float32))

        return jnp.maximum(lookup(bottom, blocks) - lookup(top, jnp.minimum(blocks, 4)), 0.0)

    def heads(low, high):
        @pl.loop(low, high)
        def _(i):
            rows = pl.ds(pl.multiple_of(i * 8, 8), 8)
            top = capv[rows, :]
            bottom = pluv[rows, :]
            above = across(table[layer * LAYERS]) - (brine_density - gas_density) * gas_sum(layer, top, bottom)
            for k in range(LAYERS):
                depth = layer * LAYERS + k
                inside = (depth >= top) & (depth < bottom)
                mass = jnp.where(inside, gas_density * thick_s[k], brine_density * thick_s[k])
                hh[k, rows, :] = gravity_scale * (above + 0.5 * mass)
                above = above + mass

    lane_last = lax.broadcasted_iota(jnp.int32, (32, COLS), 1) < COLS - 1

    def faces(low, high):
        @pl.loop(low * LAYERS, high * LAYERS)
        def _(i):
            k = i % LAYERS
            start = pl.multiple_of((i // LAYERS) * 32, 8)
            flow = cond[k, pl.ds(start, 40), :]
            head = hh[k, pl.ds(start, 40), :]
            next_flow = pltpu.roll(flow, 39, 0)[:32]
            next_head = pltpu.roll(head, 39, 0)[:32]
            flow = flow[:32]
            head = head[:32]
            rows = pl.ds(start, 32)
            face = harmonic(flow, next_flow)
            hr[k, rows, :] = face
            gr[k, rows, :] = face * (head - next_head)
            side_flow = jnp.where(lane_last, pltpu.roll(flow, COLS - 1, 1), 0.0)
            side_head = pltpu.roll(head, COLS - 1, 1)
            face = harmonic(flow, side_flow)
            hc[k, rows, :] = face
            gc[k, rows, :] = face * (head - side_head)

    def second(h, n):
        for q in range(3):
            first_copy(h, q, n)[1].wait_recv()
            copy, flip = second_copy(h, q, n)
            rows = part_rows(h, q, flip)
            tb[:, rows, :] = tb[:, rows, :] + r1[h][q][n]
            send(copy)

    def third(h):
        for q in range(3):
            first_copy(h, q, 2)[1].wait_recv()
            second_copy(h, q, 0)[0].wait_recv()
            copy, flip = third_copy(h, q)
            rows = part_rows(h, q, flip)
            tb[:, rows, :] = tb[:, rows, :] + (r1[h][q][2] + r2[h][q][0])
            send(copy)

    def final(h):
        for q in range(3):
            first_copy(h, q, 3)[1].wait_recv()
            second_copy(h, q, 1)[0].wait_recv()
            third_copy(h, q)[0].wait_recv()
            mine = part_rows(h, q, OWN)
            at = pl.ds(HALO + PART_START[h][q], PART_ROWS[h][q])
            wide[h, :, at, :] = tb[:, mine, :] + r1[h][q][3] + (r2[h][q][1] + r3[h][q][...])

    forward_up = pltpu.make_async_remote_copy(
        sums.at[0], cross.at[1], sum_send.at[0], sum_recv.at[1],
        device_id=(area - 1, layer), device_id_type=MESH,
    )
    forward_down = pltpu.make_async_remote_copy(
        sums.at[1], cross.at[0], sum_send.at[1], sum_recv.at[0],
        device_id=(area + 1, layer), device_id_type=MESH,
    )

    def forward_edges():
        for owned, pair in ((at_ends, 0), (at_middle, 1)):

            @pl.when(owned)
            def _(pair=pair):
                for m in range(7):
                    part_copy(m, pair).wait_recv()
                total = tiles[pair]
                for m in range(7):
                    total = total + parts[m]
                sums[...] = total

        @pl.when(crosses_up)
        def _():
            for copy in (forward_up, *to_up):
                copy.start()

        @pl.when(crosses_down)
        def _():
            for copy in (forward_down, *to_down):
                copy.start()

        @pl.when(area > 0)
        def _():
            row_copy(0, cond).start()

    def gas_rows(h, at):
        rows = pl.ds(at, 8)
        gas[h, rows, :] = buoyancy_scale * gas_sum(8, edge_i[h, 0, rows, :], edge_i[h, 1, rows, :])

    def halo_copies(h):
        before_layer = here.layer_at(jnp.maximum(here.order - 1, 0))
        after_layer = here.layer_at(jnp.minimum(here.order + 1, 7))
        inner = pltpu.make_async_remote_copy(
            wide.at[h, :, pl.ds(SLAB if h else HALO, HALO)],
            wide.at[h, :, pl.ds(0 if h else HALO + SLAB, HALO)],
            halo_send.at[h, 0], halo_recv.at[h, 0], device_id=(area, before_layer), device_id_type=MESH,
        )
        outer = pltpu.make_async_remote_copy(
            wide.at[h, :, pl.ds(HALO if h else SLAB, HALO)],
            wide.at[h, :, pl.ds(HALO + SLAB if h else 0, HALO)],
            halo_send.at[h, 1], halo_recv.at[h, 1], device_id=(area, after_layer), device_id_type=MESH,
        )
        return inner, outer

    def halo_start(h):
        inner, outer = halo_copies(h)

        @pl.when(here.order > 0)
        def _():
            inner.start()

        @pl.when(here.order < 7)
        def _():
            outer.start()

    def blank(h, at):
        rows = pl.ds(at, HALO)
        edge_i[h, :, rows, :] = jnp.zeros((2, HALO, COLS), jnp.int32)
        edge_f[h, 0, rows, :] = jnp.ones((HALO, COLS), jnp.float32)
        edge_f[h, 1, rows, :] = jnp.zeros((HALO, COLS), jnp.float32)
        edge_f[h, 2, rows, :] = jnp.zeros((HALO, COLS), jnp.float32)
        wide[h, :, rows, :] = jnp.zeros((2, HALO, COLS), jnp.float32)

    def unpack(h, at, tile, used):
        rows = pl.ds(at, HALO)
        wide[h, 0, rows, :] = jnp.where(used, tile, 0.0)
        wide[h, 1, rows, :] = jnp.where(used, pltpu.roll(tile, 4, 0), 0.0)

    def halo_finish(h):
        inner, outer = halo_copies(h)
        if h == 0:

            @pl.when(top_edge)
            def _():
                blank(0, 0)

            @pl.when(crosses_up)
            def _():
                for copy in (forward_down, *to_down):
                    copy.wait_recv()
                unpack(0, 0, cross[0], sub8 >= 4)

            @pl.when(at_middle)
            def _():
                unpack(0, HALO + SLAB, sums[0], sub8 < 4)

            gas_rows(0, 0)
        else:

            @pl.when(bottom_edge)
            def _():
                blank(1, HALO + SLAB)

            @pl.when(crosses_down)
            def _():
                for copy in (forward_up, *to_up):
                    copy.wait_recv()
                unpack(1, HALO + SLAB, cross[1], sub8 < 4)

            @pl.when(at_middle)
            def _():
                unpack(1, 0, sums[1], sub8 >= 4)

            gas_rows(1, HALO + SLAB)

        @pl.when(here.order > 0)
        def _():
            outer.wait_recv()

        @pl.when(here.order < 7)
        def _():
            inner.wait_recv()

    lane = lax.broadcasted_iota(jnp.int32, (WIDE, COLS), 1)

    def after(x):
        return pltpu.roll(x, WIDE - 1, 0)

    def before(x):
        return pltpu.roll(x, 1, 0)

    def right(x):
        return jnp.where(lane < COLS - 1, pltpu.roll(x, COLS - 1, 1), 0.0)

    def left(x):
        return jnp.where(lane > 0, pltpu.roll(x, 1, 1), 0.0)

    def relax(h):
        trans = wide[h, 0]
        face_row = harmonic(trans, after(trans))
        t_row[...] = face_row
        face_col = harmonic(trans, right(trans))
        t_col[...] = face_col
        diagonal = edge_f[h, 0] + face_row + before(face_row) + face_col + left(face_col)
        inverse[...] = 1.0 / diagonal
        buoy = wide[h, 1]
        drive = gas[h]
        push = harmonic(buoy, after(buoy)) * (after(drive) - drive)
        total = push - before(push)
        push = harmonic(buoy, right(buoy)) * (right(drive) - drive)
        total = total + (push - left(push))
        right_hand[...] = edge_f[h, 0] * edge_f[h, 2] + edge_f[h, 1] + total

        for sweep in range(SWEEPS):
            pressure = edge_f[h, 2]
            face_row = t_row[...]
            face_col = t_col[...]
            inflow = face_row * after(pressure) + before(face_row * pressure)
            inflow = inflow + (face_col * right(pressure) + left(face_col * pressure))
            edge_f[h, 2] = (right_hand[...] + inflow) * inverse[...]

        pf[here.rows(h, OWN, 0, SLAB), :] = edge_f[h, 2, pl.ds(HALO, SLAB), :]

    def ag_messages(h):
        def first_rows(flip):
            return here.rows(h, flip, 0, X_FIRST[h])

        def later_rows(flip):
            return here.rows(h, flip, X_FIRST[h], SLAB - X_FIRST[h])

        half_x = (0, first_rows, OWN, OTHER_HALF)
        x_own = [(1 + n, later_rows, OWN, x) for n, x in enumerate(ACROSS)]
        x_first = [(4 + n, first_rows, OWN, x) for n, x in enumerate(ACROSS)]
        half_own = (7, later_rows, OWN, OTHER_HALF)
        half_on = [(8 + n, first_rows, OTHER_HALF, x) for n, x in enumerate(ACROSS)]
        x_on = [(11 + n, later_rows, x, OTHER_HALF) for n, x in enumerate(ACROSS)]
        return half_x, x_own, x_first, half_own, half_on, x_on

    def ag_copy(h, number, rows, to):
        return pltpu.make_async_remote_copy(
            pf.at[rows], pf.at[rows], ag_send.at[h, number], ag_recv.at[h, number],
            device_id=peer(to), device_id_type=MESH,
        )

    def spread(h, number, rows_of, flip, to):
        send(ag_copy(h, number, rows_of(flip), to))

    def arrived(h, number, rows_of, flip, to):
        ag_copy(h, number, rows_of(plus(flip, to)), to).wait_recv()

    def gather_start(h):
        half_x, x_own, x_first, half_own, _, _ = ag_messages(h)
        for message in (half_x, *x_own, *x_first, half_own):
            spread(h, *message)

    def gather_pass(h):
        half_x, x_own, _, _, half_on, x_on = ag_messages(h)
        arrived(h, *half_x)
        for n in range(3):
            spread(h, *half_on[n])
        for n in (1, 2, 0):
            arrived(h, *x_own[n])
            spread(h, *x_on[n])

    def gather_finish(h):
        _, _, x_first, half_own, half_on, x_on = ag_messages(h)
        for message in (*x_first, half_own, *half_on, *x_on):
            arrived(h, *message)

    def last_copy(m, other):
        return pltpu.make_async_remote_copy(
            pf.at[pl.ds(ROWS, 8)], pf.at[pl.ds(ROWS, 8)], last_send.at[m], last_recv.at[0],
            device_id=peer(other), device_id_type=MESH,
        )

    second(0, 0)
    second(0, 1)
    for copy in later:
        send(copy)

    for m, other in enumerate(OTHERS):
        pltpu.make_async_remote_copy(
            thick_all.at[layer], thick_all.at[here.layer_of(other)], th_send.at[m], th_recv.at[m],
            device_id=peer(other), device_id_type=MESH,
        ).wait_recv()
    total = jnp.zeros((8, 128), jnp.float32)
    table[0] = total
    for block in range(8):
        for k in range(LAYERS):
            total = total + jnp.broadcast_to(thick_all[block, pl.ds(k, 1), :], (8, 128))
            table[block * LAYERS + k + 1] = total


    third(0)
    second(1, 0)
    second(1, 1)

    @pl.when(here.parity == 0)
    def _():
        pl.semaphore_wait(ready, 2)

    forward_edges()
    heads(0, 32)

    for copy in (*always[0], *always[1]):
        copy.wait()

    @pl.when(here.order > 0)
    def _():
        for h in range(HALVES):
            for copy in sometimes(h):
                copy.wait()

    @pl.loop(1, WIDE // 8)
    def _(i):
        gas_rows(0, pl.multiple_of(i * 8, 8))

    final(0)
    halo_start(0)
    third(1)

    @pl.loop(0, WIDE // 8 - 1)
    def _(i):
        gas_rows(1, pl.multiple_of(i * 8, 8))

    halo_finish(0)
    relax(0)
    gather_start(0)
    heads(32, 64)

    @pl.when(area > 0)
    def _():
        row_copy(1, hh).start()

    final(1)
    halo_start(1)
    gather_pass(0)
    halo_finish(1)
    relax(1)
    gather_start(1)

    @pl.when(at_ends)
    def _():
        pf[pl.ds(ROWS, 8), :] = edge_f[1, 2, pl.ds(HALO + SLAB, 8), :]
        for m, other in enumerate(OTHERS):
            last_copy(m, other).start()

    faces(0, 7)
    gather_pass(1)
    faces(7, 15)

    @pl.when(area < here.areas - 1)
    def _():
        row_copy(0, cond).wait_recv()
        row_copy(1, hh).wait_recv()

    @pl.when(area == here.areas - 1)
    def _():
        cond[:, pl.ds(ROWS, 8), :] = jnp.zeros((LAYERS, 8, COLS), jnp.float32)
        hh[:, pl.ds(ROWS, 8), :] = jnp.zeros((LAYERS, 8, COLS), jnp.float32)

    faces(15, 16)
    gather_finish(0)
    gather_finish(1)

    @pl.when(here.order > 0)
    def _():
        last_copy(0, OTHERS[0]).wait_recv()

    for copy in waits:
        copy.wait_send()

    @pl.when(at_ends)
    def _():
        for m, other in enumerate(OTHERS):
            last_copy(m, other).wait_send()

    for h in range(HALVES):
        inner, outer = halo_copies(h)

        @pl.when(here.order > 0)
        def _(inner=inner):
            inner.wait_send()

        @pl.when(here.order < 7)
        def _(outer=outer):
            outer.wait_send()

    @pl.when(here.order > 0)
    def _():
        part_copy(0, 0).wait_send()

    @pl.when(here.order < 7)
    def _():
        part_copy(0, 1).wait_send()

    @pl.when(area > 0)
    def _():
        row_copy(0, cond).wait_send()
        row_copy(1, hh).wait_send()

    @pl.when(crosses_up)
    def _():
        for copy in (forward_up, *to_up):
            copy.wait_send()

    @pl.when(crosses_down)
    def _():
        for copy in (forward_down, *to_down):
            copy.wait_send()


CHUNK = 32


def write_kernel(hh, hr, gr, hc, gc, pf, cell, rows_out, cols_out, cell_v, rows_v, cols_v, sems):
    chunks = ROWS // CHUNK

    def copies(i):
        rows = pl.ds(pl.multiple_of(i * CHUNK, 8), CHUNK)
        return [
            pltpu.make_async_copy(v.at[:, rows], o.at[:, rows], sems.at[n, i])
            for n, (v, o) in enumerate(((cell_v, cell), (rows_v, rows_out), (cols_v, cols_out)))
        ]

    @pl.loop(0, chunks)
    def _(i):
        start = pl.multiple_of(i * CHUNK, 8)
        rows = pl.ds(start, CHUNK)
        wide = pf[pl.ds(start, CHUNK + 8), :]
        pressure = wide[:CHUNK]
        row_drop = pressure - pltpu.roll(wide, CHUNK + 7, 0)[:CHUNK]
        col_drop = pressure - pltpu.roll(pressure, COLS - 1, 1)
        for k in range(LAYERS):
            cell_v[k, rows, :] = pressure + hh[k, rows, :]
            rows_v[k, rows, :] = hr[k, rows, :] * row_drop + gr[k, rows, :]
            cols_v[k, rows, :] = hc[k, rows, :] * col_drop + gc[k, rows, :]
        for copy in copies(i):
            copy.start()

    @pl.loop(0, chunks)
    def _(i):
        for copy in copies(i):
            copy.wait()


def local(permeability, mobility, thickness, caprock, plume, storage, source, pressure_old):
    f32, i32 = jnp.float32, jnp.int32
    vmem = pl.BlockSpec(memory_space=pltpu.VMEM)
    hbm = pl.BlockSpec(memory_space=pltpu.HBM)
    dma = pltpu.SemaphoreType.DMA
    V = pltpu.VMEM
    full = V((LAYERS, ROWS, COLS), f32)
    tall = V((LAYERS, ROWS + 8, COLS), f32)
    arrays = (permeability, mobility, thickness, caprock, plume, storage, source, pressure_old)
    arrays = [pltpu.with_memory_space_constraint(x, pltpu.HBM) for x in arrays]
    kept = pl.pallas_call(
        gather_kernel,
        out_shape=[tall, full, full, full, full, V((ROWS + 8, COLS), f32)],
        in_specs=[hbm] * 8,
        out_specs=[vmem] * 6,
        scratch_shapes=[
            *[V((4, 2, r, COLS), f32) for parts in PART_ROWS for r in parts],
            *[V((2, 2, r, COLS), f32) for parts in PART_ROWS for r in parts],
            *[V((2, r, COLS), f32) for parts in PART_ROWS for r in parts],
            V((LAYERS, ROWS, COLS), f32), V((LAYERS, ROWS, COLS), f32), V((LAYERS, ROWS + 8, COLS), f32),
            V((ROWS, COLS), i32), V((ROWS, COLS), i32), V((2, ROWS, COLS), f32),
            V((2, 4, LAYERS, 8, COLS), f32), V((2, 4, 8, COLS), i32), V((2, 2, 8, COLS), f32),
            V((7, 2, 8, COLS), f32), V((2, 8, COLS), f32), V((2, 8, COLS), f32),
            V((HALVES, 2, WIDE, COLS), f32), V((HALVES, 2, WIDE, COLS), i32), V((HALVES, 3, WIDE, COLS), f32),
            pltpu.SMEM((LAYERS,), f32), V((8, 8, 128), f32), V((33, 8, 128), f32),
            V((HALVES, WIDE, COLS), f32), *[V((WIDE, COLS), f32) for _ in range(4)],
            dma((16, 4)), dma((4, 5)), dma((1,)), dma((6, 7)), dma((6, 7)), dma((2, 14)), dma((2, 14)),
            dma((7,)), dma((7,)),
            dma((4, 4)), dma((2,)), dma((7,)), dma((2,)), dma((2,)), pltpu.SemaphoreType.REGULAR,
            dma((2, 2)), dma((2, 2)), dma((2, 5)), dma((2, 5)), dma((2,)), dma((2,)),
            dma((7,)), dma((1,)),
        ],
        compiler_params=pltpu.CompilerParams(
            collective_id=0, has_side_effects=True, vmem_limit_bytes=26 << 20
        ),
        name="gather",
    )(*arrays)
    return pl.pallas_call(
        write_kernel,
        out_shape=[jax.ShapeDtypeStruct((LAYERS, ROWS, COLS), f32)] * 3,
        in_specs=[vmem] * 6,
        out_specs=[hbm] * 3,
        scratch_shapes=[V((LAYERS, ROWS, COLS), f32)] * 3 + [dma((3, ROWS // CHUNK))],
        compiler_params=pltpu.CompilerParams(vmem_limit_bytes=16 << 20),
        name="write",
    )(*kept)


def solution(mesh):
    in_specs = (
        P("layer", "area", None),
        P("layer", "area", None),
        P("layer"),
        P("area", None),
        P("area", None),
        P("area", None),
        P("area", None),
        P("area", None),
    )
    out_specs = (P("layer", "area", None), P("layer", "area", None), P("layer", "area", None))
    return jax.shard_map(
        lambda *args: tuple(local(*args)), mesh=mesh, in_specs=in_specs, out_specs=out_specs, check_vma=False
    )
```

time: 50.9 us -> 53.5 us (1.051)
  Pallas kernels: 50.1 us -> 52.8 us
    pallas_call x1, Pallas kernels: 45.1 us -> 47.7 us  [local(): pl.pallas_call(gather_kernel, out_shape=[tall, full, full, full, full, V(...]
where the time goes in v3:
time: 53.5 us; the launch traced here: 53.4 us
  Pallas kernels  52.8 us (99%)
  between operations  0.64 us (1%)
    pallas_call x1, Pallas kernels, local(): pl.pallas_call(gather_kernel, out_shape=[tall, full, full, full, full, V(...  47.7 us
    pallas_call x1, Pallas kernels, local(): pl.pallas_call(write_kernel, out_shape=[jax.ShapeDtypeStruct((LAYERS, ROW...  5.02 us

profile of v3, /device:TPU:0, one launch (start us, length us, event | category | flops | bytes accessed | tf_op | source)
XLA Modules:
  0.0 53.4 jit_solution(3905029772821153179)
XLA Ops:
  0.6 47.7 %gather.1 = (f32[4,520,512]{2,1,0:T(8,128)S(1)}, f32[4,512,512]{2,1,0:T(8,128)S(1)}, f32[4,512,512]{2,1,0:T(8,128)S(1)}, f32[4,512,512]{2,1,0:T(8,128)S(1)}, f32...) custom-call(f32[4,512,512]{2,1,0:T(8,128)} %refs_0_.1, f32[4,512,512]{2,1,0:T(8,128)} %refs_1_.1, f32[4]{0:T(128)} %refs_2_.1, ...), custom_call_target="tpu_custom_call" | custom-call | tf_op jit(solution)/shard_map/gather/pallas_call | solution.py:792
  48.4 5.0 %write.1 = (f32[4,512,512]{2,1,0:T(8,128)}, f32[4,512,512]{2,1,0:T(8,128)}, f32[4,512,512]{2,1,0:T(8,128)}) custom-call(f32[4,520,512]{2,1,0:T(8,128)S(1)} %get-tuple-element.9.hh, f32[4,512,512]{2,1,0:T(8,128)S(1)} %get-tuple-element.10.hr, f32[4,512,512]{2,1,0:T(8,128)S(1)} %get-tuple-element.11.gr, f32[4,512,512]{2,1,0:T(8,128)S(1)} %get-tuple-element.12.hc, ...), custom_call_target="tpu_custom_call" | custom-call | tf_op jit(solution)/shard_map/write/pallas_call | solution.py:819

commit v4 on v2

--- a/solution.py
+++ b/solution.py
@@ -26,6 +26,10 @@
 PART_ROWS = (24, 24, 16)
 FLIPS = ((1, 1, 1), (1, 1, 0), (0, 1, 1), (1, 0, 1), (1, 0, 0), (0, 1, 0), (0, 0, 1), (0, 0, 0))
 OTHERS = FLIPS[:-1]
+X_FIRST = 24
+ACROSS = ((1, 1, 0), (1, 0, 0), (0, 1, 0))
+OTHER_HALF = (0, 0, 1)
+OWN = (0, 0, 0)
 
 
 def harmonic(near_value, far_value):
@@ -36,6 +40,10 @@
 
 def flip_of(*dims):
     return tuple(1 if d in dims else 0 for d in range(3))
+
+
+def plus(one, two):
+    return tuple((a + b) % 2 for a, b in zip(one, two))
 
 
 class Place:
@@ -567,25 +575,35 @@
     def _():
         pf[pl.ds(ROWS, 8), :] = edge_f[2, pl.ds(HALO + SLAB, 8), :]
 
-    def ag_copy(q, number, flip, dim):
-        rows = part_rows(q, flip)
+    def first_rows(flip):
+        return here.rows(flip, 0, X_FIRST)
+
+    def later_rows(flip):
+        return here.rows(flip, X_FIRST, SLAB - X_FIRST)
+
+    def ag_copy(number, rows, to):
         return pltpu.make_async_remote_copy(
-            pf.at[rows], pf.at[rows], ag_send.at[q, number], ag_recv.at[q, number],
-            device_id=peer(flip_of(dim)), device_id_type=MESH,
+            pf.at[rows], pf.at[rows], ag_send.at[number], ag_recv.at[number],
+            device_id=peer(to), device_id_type=MESH,
         )
 
-    def ag_arrival(q, number, flip, dim):
-        merged = tuple((a + b) % 2 for a, b in zip(flip, flip_of(dim)))
-        ag_copy(q, number, merged, dim).wait_recv()
-
-    def ag_send_one(q, number, flip, dim):
-        copy = ag_copy(q, number, flip, dim)
+    half_x = (0, first_rows, OWN, OTHER_HALF)
+    x_own = [(1 + n, later_rows, OWN, x) for n, x in enumerate(ACROSS)]
+    x_first = [(4 + n, first_rows, OWN, x) for n, x in enumerate(ACROSS)]
+    half_own = (7, later_rows, OWN, OTHER_HALF)
+    half_on = [(8 + n, first_rows, OTHER_HALF, x) for n, x in enumerate(ACROSS)]
+    x_on = [(11 + n, later_rows, x, OTHER_HALF) for n, x in enumerate(ACROSS)]
+
+    def spread(number, rows_of, flip, to):
+        copy = ag_copy(number, rows_of(flip), to)
         copy.start()
         waits.append(copy)
 
-    for which in (2, 1, 0):
-        for q in range(3):
-            ag_send_one(q, (0, 0, 0)[which] if which == 2 else (3, 1, 0)[which], (0, 0, 0), ORDERS[q][which])
+    def arrived(number, rows_of, flip, to):
+        ag_copy(number, rows_of(plus(flip, to)), to).wait_recv()
+
+    for message in (half_x, *x_own, *x_first, half_own):
+        spread(*message)
 
     def last_copy(m, other):
         return pltpu.make_async_remote_copy(
@@ -598,23 +616,14 @@
         for m, other in enumerate(OTHERS):
             last_copy(m, other).start()
 
-    faces(0, 4)
-    for q in range(3):
-        d1, d2, d3 = ORDERS[q]
-        ag_arrival(q, 0, (0, 0, 0), d3)
-        ag_send_one(q, 2, flip_of(d3), d2)
-        ag_send_one(q, 4, flip_of(d3), d1)
-    faces(4, 8)
-    for q in range(3):
-        d1, d2, d3 = ORDERS[q]
-        ag_arrival(q, 1, (0, 0, 0), d2)
-        ag_send_one(q, 5, flip_of(d2), d1)
-    faces(8, 11)
-    for q in range(3):
-        d1, d2, d3 = ORDERS[q]
-        ag_arrival(q, 2, flip_of(d3), d2)
-        ag_send_one(q, 6, flip_of(d2, d3), d1)
-    faces(11, 15)
+    faces(0, 5)
+    arrived(*half_x)
+    for n in range(3):
+        spread(*half_on[n])
+    for n in (1, 2, 0):
+        arrived(*x_own[n])
+        spread(*x_on[n])
+    faces(5, 15)
 
     @pl.when(area < here.areas - 1)
     def _():
@@ -627,10 +636,8 @@
         hh[:, pl.ds(ROWS, 8), :] = jnp.zeros((LAYERS, 8, COLS), jnp.float32)
 
     faces(15, 16)
-    for number, dims in ((3, ()), (4, (2,)), (5, (1,)), (6, (1, 2))):
-        for q in range(3):
-            order = ORDERS[q]
-            ag_arrival(q, number, flip_of(*[order[d] for d in dims]), order[0])
+    for message in (*x_first, half_own, *half_on, *x_on):
+        arrived(*message)
 
     @pl.when(here.slab < 7)
     def _():
@@ -676,7 +683,7 @@
             copy.wait_send()
 
 
-CHUNK = 32
+CHUNK = 64
 
 
 def write_kernel(hh, hr, gr, hc, gc, pf, cell, rows_out, cols_out, cell_v, rows_v, cols_v, sems):
@@ -736,7 +743,7 @@
             V((2, WIDE, COLS), f32), V((2, WIDE, COLS), i32), V((3, WIDE, COLS), f32),
             pltpu.SMEM((LAYERS,), f32), V((8, 8, 128), f32), V((33, 8, 128), f32),
             *[V((WIDE, COLS), f32) for _ in range(5)],
-            dma((8, 4)), dma((3, 5)), dma((1,)), dma((3, 7)), dma((3, 7)), dma((3, 7)), dma((3, 7)),
+            dma((8, 4)), dma((3, 5)), dma((1,)), dma((3, 7)), dma((3, 7)), dma((14,)), dma((14,)),
             dma((7,)), dma((7,)),
             dma((2, 4)), dma((2,)), dma((7,)), dma((1,)), dma((2,)), pltpu.SemaphoreType.REGULAR,
             dma((2,)), dma((2,)), dma((2, 5)), dma((2, 5)), dma((2,)), dma((2,)),

time: 50.9 us -> 49.9 us (0.980)
  Pallas kernels: 50.1 us -> 49.1 us
    pallas_call x1, Pallas kernels: 45.1 us -> 44.1 us  [local(): pl.pallas_call(gather_kernel, out_shape=[tall, full, full, full, full, V(...]
where the time goes in v4:
time: 49.9 us; the launch traced here: 49.8 us
  Pallas kernels  49.1 us (98%)
  between operations  0.64 us (1%)
    pallas_call x1, Pallas kernels, local(): pl.pallas_call(gather_kernel, out_shape=[tall, full, full, full, full, V(...  44.1 us
    pallas_call x1, Pallas kernels, local(): pl.pallas_call(write_kernel, out_shape=[jax.ShapeDtypeStruct((LAYERS, ROW...  4.98 us

profile of v4, /device:TPU:0, one launch (start us, length us, event | category | flops | bytes accessed | tf_op | source)
XLA Modules:
  0.0 49.8 jit_solution(16909217612066671762)
XLA Ops:
  0.6 44.1 %gather.1 = (f32[4,520,512]{2,1,0:T(8,128)S(1)}, f32[4,512,512]{2,1,0:T(8,128)S(1)}, f32[4,512,512]{2,1,0:T(8,128)S(1)}, f32[4,512,512]{2,1,0:T(8,128)S(1)}, f32...) custom-call(f32[4,512,512]{2,1,0:T(8,128)} %perm.1, f32[4,512,512]{2,1,0:T(8,128)} %mob.1, f32[4]{0:T(128)} %thick.1, ...), custom_call_target="tpu_custom_call" | custom-call | tf_op jit(solution)/shard_map/gather/pallas_call | solution.py:730
  44.8 5.0 %write.1 = (f32[4,512,512]{2,1,0:T(8,128)}, f32[4,512,512]{2,1,0:T(8,128)}, f32[4,512,512]{2,1,0:T(8,128)}) custom-call(f32[4,520,512]{2,1,0:T(8,128)S(1)} %get-tuple-element.9.hh, f32[4,512,512]{2,1,0:T(8,128)S(1)} %get-tuple-element.10.hr, f32[4,512,512]{2,1,0:T(8,128)S(1)} %get-tuple-element.11.gr, f32[4,512,512]{2,1,0:T(8,128)S(1)} %get-tuple-element.12.hc, ...), custom_call_target="tpu_custom_call" | custom-call | tf_op jit(solution)/shard_map/write/pallas_call | solution.py:757

commit v5 on v4

--- a/solution.py
+++ b/solution.py
@@ -285,14 +285,18 @@
         flip = flip_of(d3)
         return flip, rs_copy(q, 6, part_rows(q, flip), r3[q], d3)
 
+    held = []
     for n, flip in enumerate(FLIPS):
         conduct_slab(n, flip)
         for q in range(3):
             for m in range(4):
                 owner, copy = first_copy(q, m)
                 if owner == flip:
-                    copy.start()
                     waits.append(copy)
+                    if m == 3:
+                        held.append(copy)
+                    else:
+                        copy.start()
 
     def row_copy(n, array):
         return pltpu.make_async_remote_copy(
@@ -401,11 +405,11 @@
         rows = pl.ds(at, 8)
         gas[rows, :] = buoyancy_scale * gas_sum(8, edge_i[0, rows, :], edge_i[1, rows, :])
 
-    @pl.when(here.parity == 1)
-    def _():
-        forward_edges()
-
     second(0)
+    for copy in held:
+        copy.start()
+
+    second(1)
 
     for m, other in enumerate(OTHERS):
         pltpu.make_async_remote_copy(
@@ -420,7 +424,10 @@
             table[block * LAYERS + k + 1] = total
 
 
-    second(1)
+    @pl.when(here.parity == 1)
+    def _():
+        forward_edges()
+
     heads(0, 32)
 
     @pl.when(here.parity == 0)

time: 49.9 us -> 49.3 us (0.988)
  Pallas kernels: 49.1 us -> 48.6 us
    pallas_call x1, Pallas kernels: 44.1 us -> 43.6 us  [local(): pl.pallas_call(gather_kernel, out_shape=[tall, full, full, full, full, V(...]
where the time goes in v5:
time: 49.3 us; the launch traced here: 49.2 us
  Pallas kernels  48.6 us (99%)
  between operations  0.64 us (1%)
    pallas_call x1, Pallas kernels, local(): pl.pallas_call(gather_kernel, out_shape=[tall, full, full, full, full, V(...  43.6 us
    pallas_call x1, Pallas kernels, local(): pl.pallas_call(write_kernel, out_shape=[jax.ShapeDtypeStruct((LAYERS, ROW...  4.98 us

profile of v5, /device:TPU:0, one launch (start us, length us, event | category | flops | bytes accessed | tf_op | source)
XLA Modules:
  0.0 49.2 jit_solution(14244381046129936286)
XLA Ops:
  0.6 43.6 %gather.1 = (f32[4,520,512]{2,1,0:T(8,128)S(1)}, f32[4,512,512]{2,1,0:T(8,128)S(1)}, f32[4,512,512]{2,1,0:T(8,128)S(1)}, f32[4,512,512]{2,1,0:T(8,128)S(1)}, f32...) custom-call(f32[4,512,512]{2,1,0:T(8,128)} %perm.1, f32[4,512,512]{2,1,0:T(8,128)} %mob.1, f32[4]{0:T(128)} %thick.1, ...), custom_call_target="tpu_custom_call" | custom-call | tf_op jit(solution)/shard_map/gather/pallas_call | solution.py:737
  44.2 5.0 %write.1 = (f32[4,512,512]{2,1,0:T(8,128)}, f32[4,512,512]{2,1,0:T(8,128)}, f32[4,512,512]{2,1,0:T(8,128)}) custom-call(f32[4,520,512]{2,1,0:T(8,128)S(1)} %get-tuple-element.9.hh, f32[4,512,512]{2,1,0:T(8,128)S(1)} %get-tuple-element.10.hr, f32[4,512,512]{2,1,0:T(8,128)S(1)} %get-tuple-element.11.gr, f32[4,512,512]{2,1,0:T(8,128)S(1)} %get-tuple-element.12.hc, ...), custom_call_target="tpu_custom_call" | custom-call | tf_op jit(solution)/shard_map/write/pallas_call | solution.py:764
